TPU v7x, 32 devices: a whole 2x2x4 slice. The times are simulated.
32 devices in a mesh: partner: 8 (over y, x, core), block: 4 (over z).
Axes of the slice: x: 2, y: 2, z: 4, core: 2. Of those that a mesh axis runs over, the one named last changes fastest.
Arguments:
- points: bfloat16 [32, 32768], P(None, ('partner', 'block')), may hold values from -6 to 6
- tree_order: int32 [32768], P(('partner', 'block')), may hold values from 0 to 32767, as said below
- nearby_dense_blocks: bfloat16 [256, 3, 128, 128], P(('partner', 'block')), may hold values from -0.3125 to 0.3125
- neighbours: int32 [256, 3], P(('partner', 'block')), may hold values from 0 to 255, as said below
- compress: bfloat16 [256, 128, 128], P(('partner', 'block')), may hold values from -0.5 to 0.5
- expand: bfloat16 [256, 128, 128], P(('partner', 'block')), may hold values from -0.5 to 0.5
- top_factor: bfloat16 [256, 128, 128], P(('partner', 'block')), may hold values from -0.5 to 0.5
- butterfly_mixers: bfloat16 [2, 256, 2, 128, 128], P(None, ('partner', 'block')), may hold values from -0.375 to 0.375
- block_map: int32 [3, 8], replicated, may hold values from 0 to 7, as said below
Outputs:
- applied: bfloat16 [32, 32768], P(None, ('partner', 'block'))
Inputs may be any that keep to these rules, and one draw needn't show every extreme that they name: tree_order[r] lies among the 1024 points of the aligned group of 1024 rows that holds r, and names every point once. neighbours[l, 0] is l; every other entry lies within 2 leaves of l and in the same aligned group of 32 leaves as l. `block_map`: each row names exactly 4 different slots, each of them twice.
All inputs are finite; a program needn't handle non-finite values.
Results may differ from a plain program's by a relative error of at most 0.001.
Values may be sent and summed in bfloat16 or wider, within the bound.
No kernel may reach another device: no remote copies, remote signals or barrier semaphores. Data moves between devices by JAX's collectives and lax.ppermute only.
A program may use at most 64 MiB of HBM per device.

v0:
```python
import jax
import jax.numpy as jnp
from jax import lax
from jax.sharding import PartitionSpec as P

REACH = 2


HI = lax.Precision.HIGHEST


def padded_2(cells, sides, width):
    for axis, dim in sides:
        count = lax.axis_size(axis)
        ends = count - 1
        head = lax.slice_in_dim(cells, 0, width, axis=dim)
        tail = lax.slice_in_dim(cells, cells.shape[dim] - width, cells.shape[dim], axis=dim)
        cells = jnp.concatenate(
            [
                lax.ppermute(tail, axis, [(i, (i + 1) % count) for i in range(ends)]),
                cells,
                lax.ppermute(head, axis, [((i + 1) % count, i) for i in range(ends)]),
            ],
            axis=dim,
        )
    return cells


def from_partner(x, axis, bit):
    return lax.ppermute(x, axis, [(i, i ^ 1 << bit) for i in range(lax.axis_size(axis))])


def partner_piece(state, row):
    return (state, row)


def mixed_pair(own, across_partners, factor):
    widened = factor.astype(jnp.float32)
    first = jnp.einsum("bvk,bkj->bvj", own, widened[:, 0], precision=HI)
    second = jnp.einsum("bvk,bkj->bvj", across_partners, widened[:, 1], precision=HI)
    return first + second


def on_device(
    points,
    tree_order,
    nearby_dense_blocks,
    neighbours,
    compress,
    expand,
    top_factor,
    butterfly_mixers,
    block_map,
):
    vectors = points.shape[0]
    count_pts = points.shape[1]
    leaf = nearby_dense_blocks.shape[2]
    leaves = count_pts // leaf
    near_count = neighbours.shape[1]
    device = lax.axis_index("partner") * lax.axis_size("block") + lax.axis_index("block")
    local_order = tree_order - device * count_pts
    ordered = jnp.take(points, local_order, axis=1)
    padded = padded_2(ordered, (("block", 1),), REACH * leaf)
    windows = padded.reshape(vectors, leaves + 2 * REACH, leaf)
    slots = neighbours - device * leaves + REACH
    source_points = jnp.take(windows, slots.reshape(-1), axis=1).reshape(
        vectors, leaves, near_count, leaf
    )
    nearby_field_sum = jnp.einsum(
        "zxqc,xqcf->zxf", source_points, nearby_dense_blocks, preferred_element_type=jnp.float32
    )
    leaf_rows = ordered.reshape(vectors, leaves, leaf)
    state = jnp.einsum("vbs,bsk->bvk", leaf_rows, compress, preferred_element_type=jnp.float32)
    levels = lax.axis_size("partner").bit_length() - 1
    sent, row = partner_piece(state, block_map[0])
    received = from_partner(sent, "partner", levels - 1)
    across_partners = jnp.take(received, row, axis=0)
    state = jnp.einsum(
        "bvk,bkj->bvj", across_partners, top_factor.astype(jnp.float32), precision=HI
    )
    for section in range(levels - 1):
        bit = levels - 2 - section
        sent, row = partner_piece(state, block_map[section + 1])
        received = from_partner(sent, "partner", bit)
        across_partners = jnp.take(received, row, axis=0)
        state = mixed_pair(state, across_partners, butterfly_mixers[section])
    far_field = jnp.einsum("bvk,bks->vbs", state, expand.astype(jnp.float32), precision=HI)
    in_tree = (nearby_field_sum + far_field).reshape(vectors, count_pts).astype(jnp.bfloat16)
    return jnp.zeros_like(points).at[:, local_order].set(in_tree)


def solution(mesh):
    return jax.shard_map(
        on_device,
        mesh=mesh,
        in_specs=(
            P(None, ("partner", "block")),
            P(("partner", "block")),
            P(("partner", "block"), None, None, None),
            P(("partner", "block"), None),
            P(("partner", "block"), None, None),
            P(("partner", "block"), None, None),
            P(("partner", "block"), None, None),
            P(None, ("partner", "block"), None, None, None),
            P(),
        ),
        out_specs=P(None, ("partner", "block")),
        check_vma=False,
    )
```

profile of v0, /device:TPU:0, one launch (start us, length us, event | category | flops | bytes accessed | tf_op | source)
XLA Modules:
  0.0 37.0 jit_solution(16120784730877049306)
XLA Ops:
  0.0 1.1 %copy.38 = bf16[32,1024]{0,1:T(8,128)(2,1)S(1)} copy(bf16[32,1024]{1,0:T(8,128)(2,1)} %param.11) | data formatting | bytes 131072 | tf_op args[0]
  1.1 0.0 copy-start.6
  1.1 0.7 %copy-done.6 = s32[1024]{0:T(1024)S(1)} copy-done((s32[1024]{0:T(1024)S(1)}, s32[1024]{0:T(1024)}, u32[]{:S(2)}) %copy-start.6) | copy-done | bytes 4120
  1.8 0.0 copy-start.1
  1.8 3.2 %gather_fusion = bf16[1024,32]{1,0:T(8,128)(2,1)S(1)} fusion(bf16[32,1024]{0,1:T(8,128)(2,1)S(1)} %copy.38, s32[1024]{0:T(1024)S(1)} %broadcast_clamp_fusion), kind=kCustom, calls=%fused_computation.3 | custom fusion | bytes 135168 | tf_op jit(solution)/shard_map/jit(_take)/gather | solution.py:62
  5.0 0.2 bitcast_select_fusion
  5.2 0.0 copy-start.2
  5.2 0.6 %fusion.30 = (bf16[32,256]{0,1:T(8,128)(2,1)}, bf16[32,256]{0,1:T(8,128)(2,1)}) fusion(bf16[32,1024]{0,1:T(8,128)(2,1)S(1)} %bitcast_select_fusion), kind=kLoop, calls=%fused_computation.67 | loop fusion | bytes 65536 | tf_op jit(solution)/shard_map/slice | solution.py:17
  5.9 1.3 %collective-permute-start.1 = (bf16[32,256]{0,1:T(8,128)(2,1)}, bf16[32,256]{0,1:T(8,128)(2,1)}, u32[]{:S(2)}, u32[]{:S(2)}) collective-permute-start(bf16[32,256]{0,1:T(8,128)(2,1)} %get-tuple-element.17), channel_id=1, source_target_pairs={{1,0},{2,1},{3,2},{5,4},{6,5},{7,6},{9,8},{10,9},{11,10},{13,12},{... | collective-permute-start | bytes 49160 | tf_op jit(solution)/shard_map/ppermute | solution.py:22
  7.2 6.2 %collective-permute-start = (bf16[32,256]{0,1:T(8,128)(2,1)}, bf16[32,256]{0,1:T(8,128)(2,1)}, u32[]{:S(2)}, u32[]{:S(2)}) collective-permute-start(bf16[32,256]{0,1:T(8,128)(2,1)} %get-tuple-element.16), channel_id=1, source_target_pairs={{0,1},{1,2},{2,3},{4,5},{5,6},{6,7},{8,9},{9,10},{10,11},{12,13},{... | collective-permute-start | bytes 49160 | tf_op jit(solution)/shard_map/ppermute | solution.py:20
  13.4 0.1 copy.44
  13.5 0.0 copy-start.5
  13.5 0.2 fusion.16
  13.7 2.0 %collective-permute-start.2 = (f32[8,32,128]{2,1,0:T(8,128)S(1)}, f32[8,32,128]{2,1,0:T(8,128)}, u32[]{:S(2)}, u32[]{:S(2)}) collective-permute-start(f32[8,32,128]{2,1,0:T(8,128)S(1)} %fusion.16), channel_id=1, source_target_pairs={{0,16},{4,20},{8,24},{12,28},{16,0},{20,4},{24,8},{28,12},{1,17},{... | collective-permute-start | bytes 393224 | tf_op jit(solution)/shard_map/ppermute | solution.py:30
  15.7 0.1 copy.42
  15.8 0.1 reshape.62
  15.9 0.7 %copy-done.9 = s32[3,8]{1,0:T(4,128)S(1)} copy-done((s32[3,8]{1,0:T(4,128)S(1)}, s32[3,8]{1,0:T(4,128)}, u32[]{:S(2)}) %copy-start.9) | copy-done | bytes 120
  16.6 0.6 %compare_and_fusion.1 = (pred[8]{0:T(512)(128)(4,1)}, s32[8]{0:T(128)S(1)}, pred[8]{0:T(512)(128)(4,1)S(1)}, s32[8]{0:T(128)S(1)}, pred[8]{0:T(512)(128)(4,1)}, /*index=5*/s32[8]{0:T(128)S(1)}) fusion(s32[3,8]{1,0:T(4,128)S(1)} %copy-done.9), kind=kLoop, calls=%fused_computation.55 | loop fusion | flops 144 | bytes 216 | tf_op jit(solution)/shard_map/jit(_take)/and | solution.py:85
  17.2 0.1 fusion.29
  17.3 0.1 copy.40
  17.4 0.1 copy.37
  17.6 0.0 collective-permute-done.1
  17.7 0.9 %copy.41 = bf16[32,256]{1,0:T(8,128)(2,1)S(1)} copy(bf16[32,256]{0,1:T(8,128)(2,1)} %collective-permute-done.1) | data formatting | bytes 32768 | tf_op jit(solution)/shard_map/ppermute | solution.py:22
  18.6 0.0 collective-permute-done
  18.6 0.9 %copy.39 = bf16[32,256]{1,0:T(8,128)(2,1)S(1)} copy(bf16[32,256]{0,1:T(8,128)(2,1)} %collective-permute-done) | data formatting | bytes 32768 | tf_op jit(solution)/shard_map/ppermute | solution.py:20
  19.5 0.6 %gather_fusion.1 = bf16[24,32,128]{2,1,0:T(8,128)(2,1)S(1)} fusion(bf16[32,12,128]{2,0,1:T(8,128)(2,1)S(1)} %copy_bitcast_fusion.2, s32[1024]{0:T(1024)S(1)} %pad_clamp_fusion.3), kind=kCustom, calls=%fused_computation.4 | custom fusion | bytes 393312 | tf_op jit(solution)/shard_map/jit(_take)/gather | solution.py:66
  20.1 0.3 convolution_bitcast_fusion
  20.4 0.0 copy-start.3
  20.4 0.0 collective-permute-done.2
  20.5 1.5 %gather_fusion.2 = f32[8,32,128]{2,1,0:T(8,128)S(1)} fusion(f32[8,32,128]{2,1,0:T(8,128)} %collective-permute-done.2, s32[1024]{0:T(1024)S(1)} %pad_clamp_fusion.2), kind=kCustom, calls=%fused_computation.clone | custom fusion | bytes 262176 | tf_op jit(solution)/shard_map/jit(_take)/gather | solution.py:77
  22.0 0.4 %fusion.8 = f32[8,32,128]{2,1,0:T(8,128)S(1)} fusion(bf16[8,128,128]{2,1,0:T(8,128)(2,1)S(1)} %copy-done.3, f32[8,32,128]{2,1,0:T(8,128)S(1)} %gather_fusion.2, pred[8]{0:T(512)(128)(4,1)S(1)} %get-tuple-element.18), kind=kOutput, calls=%fused_computation.25 | convolution fusion | flops 50364416 | bytes 524296 | tf_op jit(solution)/shard_map/bvk,bkj->bvj/dot_general | solution.py:78
  22.4 1.6 %collective-permute-start.3 = (f32[8,32,128]{2,1,0:T(8,128)S(1)}, f32[8,32,128]{2,1,0:T(8,128)S(1)}, u32[]{:S(2)}, u32[]{:S(2)}) collective-permute-start(f32[8,32,128]{2,1,0:T(8,128)S(1)} %fusion.8), channel_id=1, source_target_pairs={{0,8},{4,12},{8,0},{12,4},{16,24},{20,28},{24,16},{28,20},{1,9},{5... | collective-permute-start | bytes 393224 | tf_op jit(solution)/shard_map/ppermute | solution.py:30
  23.9 0.3 fusion.3
  24.2 3.2 %collective-permute-done.3 = f32[8,32,128]{2,1,0:T(8,128)S(1)} collective-permute-done((f32[8,32,128]{2,1,0:T(8,128)S(1)}, f32[8,32,128]{2,1,0:T(8,128)S(1)}, u32[]{:S(2)}, u32[]{:S(2)}) %collective-permute-start.3) | collective-permute-done | bytes 131104 | tf_op jit(solution)/shard_map/ppermute | solution.py:30
  27.4 0.6 %gather_fusion.3 = f32[8,32,128]{2,1,0:T(8,128)S(1)} fusion(f32[8,32,128]{2,1,0:T(8,128)S(1)} %collective-permute-done.3, s32[1024]{0:T(1024)S(1)} %pad_clamp_fusion.1), kind=kCustom, calls=%fused_computation.1.clone | custom fusion | bytes 262176 | tf_op jit(solution)/shard_map/jit(_take)/gather | solution.py:85
  28.0 0.6 %copy-done.8 = pred[8]{0:T(512)(128)(4,1)S(1)} copy-done((pred[8]{0:T(512)(128)(4,1)S(1)}, pred[8]{0:T(512)(128)(4,1)}, u32[]{:S(2)}) %copy-start.8) | copy-done | bytes 32
  28.5 0.4 %convolution_add_fusion.2 = f32[8,32,128]{2,1,0:T(8,128)S(1)} fusion(f32[8,32,128]{2,1,0:T(8,128)S(1)} %fusion.3, bf16[8,2,128,128]{3,2,0,1:T(8,128)(2,1)S(1)} %bitcast.64, f32[8,32,128]{2,1,0:T(8,128)S(1)} %gather_fusion.3, pred[8]{0:T(512)(128)(4,1)S(1)} %copy-done.8), kind=kOutput, calls=%fused_computation.8 | convolution fusion | flops 50397184 | bytes 655872 | tf_op jit(solution)/shard_map/bvk,bkj->bvj/dot_general | solution.py:40
  28.9 0.1 collective-permute-start.4
  29.0 0.3 fusion.2
  29.3 1.0 %collective-permute-done.4 = f32[8,32,128]{2,1,0:T(8,128)S(1)} collective-permute-done((f32[8,32,128]{2,1,0:T(8,128)S(1)}, f32[8,32,128]{2,1,0:T(8,128)S(1)}, u32[]{:S(2)}, u32[]{:S(2)}) %collective-permute-start.4) | collective-permute-done | bytes 131104 | tf_op jit(solution)/shard_map/ppermute | solution.py:30
  30.3 0.6 %gather_fusion.4 = f32[8,32,128]{2,1,0:T(8,128)S(1)} fusion(f32[8,32,128]{2,1,0:T(8,128)S(1)} %collective-permute-done.4, s32[1024]{0:T(1024)S(1)} %pad_clamp_fusion), kind=kCustom, calls=%fused_computation.2.clone | custom fusion | bytes 262176 | tf_op jit(solution)/shard_map/jit(_take)/gather | solution.py:85
  30.9 0.7 %copy-done.7 = pred[8]{0:T(512)(128)(4,1)S(1)} copy-done((pred[8]{0:T(512)(128)(4,1)S(1)}, pred[8]{0:T(512)(128)(4,1)}, u32[]{:S(2)}) %copy-start.7) | copy-done | bytes 32
  31.6 0.4 %convolution_add_fusion.1 = f32[8,32,128]{2,1,0:T(8,128)S(1)} fusion(f32[8,32,128]{2,1,0:T(8,128)S(1)} %fusion.2, bf16[8,2,128,128]{3,2,0,1:T(8,128)(2,1)S(1)} %bitcast.62, f32[8,32,128]{2,1,0:T(8,128)S(1)} %gather_fusion.4, pred[8]{0:T(512)(128)(4,1)S(1)} %copy-done.7), kind=kOutput, calls=%fused_computation.7 | convolution fusion | flops 50397184 | bytes 655872 | tf_op jit(solution)/shard_map/bvk,bkj->bvj/dot_general | solution.py:40
  31.9 0.6 %copy-done.4 = bf16[8,128,128]{2,1,0:T(8,128)(2,1)S(1)} copy-done((bf16[8,128,128]{2,1,0:T(8,128)(2,1)S(1)}, bf16[8,128,128]{2,1,0:T(8,128)(2,1)}, u32[]{:S(2)}) %copy-start.4) | copy-done | bytes 262168
  32.5 0.3 fusion.1
  32.9 0.2 copy.48
  33.0 3.2 %scatter_custom_fusion = bf16[32,1024]{0,1:T(8,128)(2,1)S(1)} fusion(s32[1024]{0:T(1024)S(1)} %get-tuple-element.13, bf16[1024,32]{1,0:T(8,128)(2,1)S(1)} %copy.48, bf16[]{:T(256)} %constant.26.clone.1), kind=kCustom, calls=%fused_computation.27 | custom fusion | bytes 65538 | tf_op jit(solution)/shard_map/scatter | solution.py:89
  36.3 0.8 %copy.49 = bf16[32,1024]{1,0:T(8,128)(2,1)} copy(bf16[32,1024]{0,1:T(8,128)(2,1)S(1)} %scatter_custom_fusion) | data formatting | bytes 131072 | tf_op jit(solution)/shard_map/scatter | solution.py:89
  (23 shorter events, 0.2 us)
Async XLA Ops:
  0.0 20.1 %copy-start = (bf16[8,3,128,128]{3,2,1,0:T(8,128)(2,1)S(1)}, bf16[8,3,128,128]{3,2,1,0:T(8,128)(2,1)}, u32[]{:S(2)}) copy-start(bf16[8,3,128,128]{3,2,1,0:T(8,128)(2,1)} %param.13) | copy-start | bytes 2359300
  1.1 0.7 %copy-start.6 = (s32[1024]{0:T(1024)S(1)}, s32[1024]{0:T(1024)}, u32[]{:S(2)}) copy-start(s32[1024]{0:T(1024)} %param.12) | copy-start | bytes 12292
  1.8 15.4 %copy-start.1 = (bf16[2,8,2,128,128]{4,3,2,1,0:T(8,128)(2,1)S(1)}, bf16[2,8,2,128,128]{4,3,2,1,0:T(8,128)(2,1)}, u32[]{:S(2)}) copy-start(bf16[2,8,2,128,128]{4,3,2,1,0:T(8,128)(2,1)} %param.18) | copy-start | bytes 3145732
  5.2 8.3 %copy-start.2 = (bf16[8,128,128]{2,1,0:T(8,128)(2,1)S(1)}, bf16[8,128,128]{2,1,0:T(8,128)(2,1)}, u32[]{:S(2)}) copy-start(bf16[8,128,128]{2,1,0:T(8,128)(2,1)} %param.15) | copy-start | bytes 786436
  5.9 11.8 %collective-permute-start.1 = (bf16[32,256]{0,1:T(8,128)(2,1)}, bf16[32,256]{0,1:T(8,128)(2,1)}, u32[]{:S(2)}, u32[]{:S(2)}) collective-permute-start(bf16[32,256]{0,1:T(8,128)(2,1)} %get-tuple-element.17), channel_id=1, source_target_pairs={{1,0},{2,1},{3,2},{5,4},{6,5},{7,6},{9,8},{10,9},{11,10},{13,12},{... | collective-permute-start | bytes 49160 | tf_op jit(solution)/shard_map/ppermute | solution.py:22
  7.2 11.4 %collective-permute-start = (bf16[32,256]{0,1:T(8,128)(2,1)}, bf16[32,256]{0,1:T(8,128)(2,1)}, u32[]{:S(2)}, u32[]{:S(2)}) collective-permute-start(bf16[32,256]{0,1:T(8,128)(2,1)} %get-tuple-element.16), channel_id=1, source_target_pairs={{0,1},{1,2},{2,3},{4,5},{5,6},{6,7},{8,9},{9,10},{10,11},{12,13},{... | collective-permute-start | bytes 49160 | tf_op jit(solution)/shard_map/ppermute | solution.py:20
  13.5 2.2 %copy-start.5 = (s32[8,3]{0,1:T(4,128)S(1)}, s32[8,3]{0,1:T(4,128)}, u32[]{:S(2)}) copy-start(s32[8,3]{0,1:T(4,128)} %param.14) | copy-start | bytes 292
  13.7 6.7 %collective-permute-start.2 = (f32[8,32,128]{2,1,0:T(8,128)S(1)}, f32[8,32,128]{2,1,0:T(8,128)}, u32[]{:S(2)}, u32[]{:S(2)}) collective-permute-start(f32[8,32,128]{2,1,0:T(8,128)S(1)} %fusion.16), channel_id=1, source_target_pairs={{0,16},{4,20},{8,24},{12,28},{16,0},{20,4},{24,8},{28,12},{1,17},{... | collective-permute-start | bytes 393224 | tf_op jit(solution)/shard_map/ppermute | solution.py:30
  15.9 0.7 %copy-start.9 = (s32[3,8]{1,0:T(4,128)S(1)}, s32[3,8]{1,0:T(4,128)}, u32[]{:S(2)}) copy-start(s32[3,8]{1,0:T(4,128)} %param.19) | copy-start | bytes 292
  20.4 1.5 %copy-start.3 = (bf16[8,128,128]{2,1,0:T(8,128)(2,1)S(1)}, bf16[8,128,128]{2,1,0:T(8,128)(2,1)}, u32[]{:S(2)}) copy-start(bf16[8,128,128]{2,1,0:T(8,128)(2,1)} %param.17) | copy-start | bytes 786436
  22.4 5.0 %collective-permute-start.3 = (f32[8,32,128]{2,1,0:T(8,128)S(1)}, f32[8,32,128]{2,1,0:T(8,128)S(1)}, u32[]{:S(2)}, u32[]{:S(2)}) collective-permute-start(f32[8,32,128]{2,1,0:T(8,128)S(1)} %fusion.8), channel_id=1, source_target_pairs={{0,8},{4,12},{8,0},{12,4},{16,24},{20,28},{24,16},{28,20},{1,9},{5... | collective-permute-start | bytes 393224 | tf_op jit(solution)/shard_map/ppermute | solution.py:30
  27.9 0.6 %copy-start.8 = (pred[8]{0:T(512)(128)(4,1)S(1)}, pred[8]{0:T(512)(128)(4,1)}, u32[]{:S(2)}) copy-start(pred[8]{0:T(512)(128)(4,1)} %get-tuple-element.20) | copy-start | bytes 28
  28.9 1.4 %collective-permute-start.4 = (f32[8,32,128]{2,1,0:T(8,128)S(1)}, f32[8,32,128]{2,1,0:T(8,128)S(1)}, u32[]{:S(2)}, u32[]{:S(2)}) collective-permute-start(f32[8,32,128]{2,1,0:T(8,128)S(1)} %convolution_add_fusion.2), channel_id=1, source_target_pairs={{0,4},{4,0},{8,12},{12,8},{16,20},{20,16},{24,28},{28,24},{1,5},{5... | collective-permute-start | bytes 393224 | tf_op jit(solution)/shard_map/ppermute | solution.py:30
  30.9 0.7 %copy-start.7 = (pred[8]{0:T(512)(128)(4,1)S(1)}, pred[8]{0:T(512)(128)(4,1)}, u32[]{:S(2)}) copy-start(pred[8]{0:T(512)(128)(4,1)} %get-tuple-element.6) | copy-start | bytes 28
  31.6 0.9 %copy-start.4 = (bf16[8,128,128]{2,1,0:T(8,128)(2,1)S(1)}, bf16[8,128,128]{2,1,0:T(8,128)(2,1)}, u32[]{:S(2)}) copy-start(bf16[8,128,128]{2,1,0:T(8,128)(2,1)} %param.16) | copy-start | bytes 786436
where the time goes:
time: 37.4 us; the launch traced here: 37 us
  local copies, waits for them, and re-layouts  18 us (48%)
  starting transfers between devices  11.1 us (30%)
  waiting for transfers between devices  4.2 us (11%)
  matrix products  2.54 us (7%)
  other arithmetic  0.88 us (2%)
    ppermute x1, starting transfers between devices, padded_2(): lax.ppermute(tail, axis, [(i, (i + 1) % count) for i in range(ends)])  6.21 us
    unnamed x23, local copies, waits for them, and re-layouts  4.35 us
    ppermute x3, waiting for transfers between devices, from_partner(): lax.ppermute(x, axis, [(i, i ^ 1 << bit) for i in range(lax.axis_size(axi...  4.18 us
    scatter x2, local copies, waits for them, and re-layouts, on_device(): return jnp.zeros_like(points).at[:, local_order].set(in_tree)  3.98 us
    ppermute x3, starting transfers between devices, from_partner(): lax.ppermute(x, axis, [(i, i ^ 1 << bit) for i in range(lax.axis_size(axi...  3.62 us
    gather x2, local copies, waits for them, and re-layouts, on_device(): ordered = jnp.take(points, local_order, axis=1)  3.33 us
    gather x3, local copies, waits for them, and re-layouts, on_device(): across_partners = jnp.take(received, row, axis=0)  2.61 us
    ppermute x1, starting transfers between devices, padded_2(): lax.ppermute(head, axis, [((i + 1) % count, i) for i in range(ends)])  1.28 us
  transfers between devices with their start and end apart: 5, of which 2 were waited for; matrix products, arithmetic and copies ran while one was open for 13% of the time, Pallas kernels for 0%

commit v1 on v0

v1 whole, which is shorter than its diff:
```python
import functools

import jax
import jax.numpy as jnp
from jax import lax
from jax.experimental import pallas as pl
from jax.experimental.pallas import tpu as pltpu
from jax.sharding import PartitionSpec as P

REACH = 2
LANES = 128
VMEM = pl.BlockSpec(memory_space=pltpu.VMEM)
SMEM = pl.BlockSpec(memory_space=pltpu.SMEM)
ANY = pl.BlockSpec(memory_space=pl.ANY)


def call(body, outs, in_specs, scratch=(), flops=1 << 20, moved=1 << 18, name=None):
    single = not isinstance(outs, (list, tuple))
    return pl.pallas_call(
        body,
        out_shape=outs,
        in_specs=in_specs,
        out_specs=VMEM if single else [VMEM] * len(outs),
        scratch_shapes=list(scratch),
        compiler_params=pltpu.CompilerParams(vmem_limit_bytes=16 << 20),
        cost_estimate=pl.CostEstimate(flops=flops, bytes_accessed=moved, transcendentals=0),
        name=name,
    )


def tables(map_ref, row, slot_ref, rank_ref, slots):
    mask = jnp.int32(0)
    for i in range(slots):
        mask = mask | (jnp.int32(1) << map_ref[row, i])
    rank = jnp.int32(0)
    for j in range(slots):
        slot_ref[rank] = jnp.int32(j)
        rank_ref[j] = rank
        rank = rank + ((mask >> j) & 1)


def split(x):
    high = x.astype(jnp.bfloat16)
    low = (x - high.astype(jnp.float32)).astype(jnp.bfloat16)
    return jnp.concatenate([high, low], axis=0)


def times(pair, factor):
    both = jnp.dot(pair, factor, preferred_element_type=jnp.float32)
    rows = both.shape[0] // 2
    return both[:rows] + both[rows:]


def pick_lanes(blocks, high, low):
    rows = blocks[0].shape[0]
    high = jnp.broadcast_to(high, (rows, LANES))
    low = jnp.broadcast_to(low, (rows, LANES))
    out = jnp.take_along_axis(blocks[0], low, axis=1)
    for b in range(1, len(blocks)):
        out = jnp.where(high == b, jnp.take_along_axis(blocks[b], low, axis=1), out)
    return out


def column_blocks(x, leaves):
    return [x[:, b * LANES : (b + 1) * LANES].astype(jnp.float32) for b in range(leaves)]


def first_body(points, order, compress, block_map, sent, pts, idx, comp, table, slot, rank, sems):
    leaves = idx.shape[0]
    copies = [
        pltpu.make_async_copy(block_map, table, sems.at[0]),
        pltpu.make_async_copy(order, idx, sems.at[1]),
        pltpu.make_async_copy(points, pts, sems.at[2]),
        pltpu.make_async_copy(compress, comp, sems.at[3]),
    ]
    for copy in copies:
        copy.start()
    copies[0].wait()
    tables(table, 0, slot, rank, leaves)
    copies[1].wait()
    copies[2].wait()
    blocks = column_blocks(pts[...], leaves)
    rows = []
    for k in range(leaves // 2):
        local = idx[pl.ds(slot[k], 1), :] & (leaves * LANES - 1)
        rows.append(pick_lanes(blocks, local >> 7, local & (LANES - 1)).astype(jnp.bfloat16))
    copies[3].wait()
    for k in range(leaves // 2):
        sent[k] = split(jnp.dot(rows[k], comp[slot[k]], preferred_element_type=jnp.float32))


def order_body(points, order, ordered, head, tail):
    leaves = order.shape[0]
    blocks = column_blocks(points[...], leaves)
    for leaf in range(leaves):
        local = order[pl.ds(leaf, 1), :] & (leaves * LANES - 1)
        rows = pick_lanes(blocks, local >> 7, local & (LANES - 1)).astype(jnp.bfloat16)
        ordered[leaf] = rows
        if leaf < REACH:
            head[leaf] = rows
        if leaf >= leaves - REACH:
            tail[leaf - leaves + REACH] = rows


def near_body(base, near, before, ordered, after, blocks, order, field, place, windows):
    leaves, near_count = blocks.shape[0], blocks.shape[1]
    windows[pl.ds(0, REACH)] = before[...]
    windows[pl.ds(REACH, leaves)] = ordered[...]
    windows[pl.ds(REACH + leaves, REACH)] = after[...]
    for leaf in range(leaves):
        total = None
        for n in range(near_count):
            source = windows[near[leaf, n] - base[0] + REACH]
            term = jnp.dot(source, blocks[leaf, n], preferred_element_type=jnp.float32)
            total = term if total is None else total + term
        field[leaf] = total
    count = leaves * LANES
    target = lax.broadcasted_iota(jnp.int32, (count, LANES), 0)
    kind = lax.broadcasted_iota(jnp.int32, (8, LANES), 0)
    lane = lax.broadcasted_iota(jnp.int32, (8, LANES), 1)
    total = None
    for leaf in range(leaves):
        local = order[pl.ds(leaf, 1), :] & (count - 1)
        hit = jnp.where(target == local, 1.0, 0.0).astype(jnp.bfloat16)
        value = jnp.where(kind == 0, leaf, lane).astype(jnp.float32).astype(jnp.bfloat16)
        term = lax.dot_general(
            value, hit, (((1,), (1,)), ((), ())), preferred_element_type=jnp.float32
        )
        total = term if total is None else total + term
    place[...] = total.astype(jnp.int32)


def top_send_body(block_map, received, factor, sent, slot, rank, slot_next, rank_next):
    leaves = factor.shape[0]
    tables(block_map, 0, slot, rank, leaves)
    tables(block_map, 1, slot_next, rank_next, leaves)
    for k in range(leaves // 2):
        i = slot_next[k]
        sent[k] = split(times(received[rank[block_map[0, i]]], factor[i]))


def top_own_body(block_map, received, factor, mixers, own, slot, rank):
    leaves = factor.shape[0]
    tables(block_map, 0, slot, rank, leaves)
    for i in range(leaves):
        state = split(times(received[rank[block_map[0, i]]], factor[i]))
        own[i] = times(state, mixers[0, i, 0])


def mix_send_body(level, block_map, received, own, mixers, sent, slot, rank, slot_next, rank_next):
    leaves = own.shape[0]
    tables(block_map, level, slot, rank, leaves)
    tables(block_map, level + 1, slot_next, rank_next, leaves)
    for k in range(leaves // 2):
        i = slot_next[k]
        other = times(received[rank[block_map[level, i]]], mixers[level - 1, i, 1])
        sent[k] = split(own[i] + other)


def mix_own_body(level, block_map, received, own, mixers, own_next, slot, rank):
    leaves = own.shape[0]
    tables(block_map, level, slot, rank, leaves)
    for i in range(leaves):
        other = times(received[rank[block_map[level, i]]], mixers[level - 1, i, 1])
        own_next[i] = times(split(own[i] + other), mixers[level, i, 0])


def last_body(level, block_map, received, own, mixers, expand, field, place, applied, slot, rank):
    leaves = own.shape[0]
    tables(block_map, level, slot, rank, leaves)
    blocks = []
    for i in range(leaves):
        other = times(received[rank[block_map[level, i]]], mixers[level - 1, i, 1])
        far = times(split(own[i] + other), expand[i])
        blocks.append((field[i] + far).astype(jnp.bfloat16).astype(jnp.float32))
    for b in range(leaves):
        high = place[pl.ds(0, 1), b * LANES : (b + 1) * LANES]
        low = place[pl.ds(1, 1), b * LANES : (b + 1) * LANES]
        applied[:, b * LANES : (b + 1) * LANES] = pick_lanes(blocks, high, low).astype(jnp.bfloat16)


def from_partner(x, axis, bit):
    return lax.ppermute(x, axis, [(i, i ^ 1 << bit) for i in range(lax.axis_size(axis))])


def on_device(
    points,
    tree_order,
    nearby_dense_blocks,
    neighbours,
    compress,
    expand,
    top_factor,
    butterfly_mixers,
    block_map,
):
    vectors, count = points.shape
    leaves = nearby_dense_blocks.shape[0]
    levels = lax.axis_size("partner").bit_length() - 1
    half = leaves // 2
    device = lax.axis_index("partner") * lax.axis_size("block") + lax.axis_index("block")
    base = (device * leaves).astype(jnp.int32).reshape(1)
    order = tree_order.reshape(leaves, LANES)
    ints = pltpu.SMEM((leaves + 1,), jnp.int32)
    pair = jax.ShapeDtypeStruct((half, 2 * vectors, LANES), jnp.bfloat16)
    state = jax.ShapeDtypeStruct((leaves, vectors, LANES), jnp.float32)
    edge = jax.ShapeDtypeStruct((REACH, vectors, LANES), jnp.bfloat16)

    sent = call(
        first_body,
        pair,
        [ANY, ANY, ANY, ANY],
        [
            pltpu.VMEM(points.shape, points.dtype),
            pltpu.VMEM(order.shape, order.dtype),
            pltpu.VMEM(compress.shape, compress.dtype),
            pltpu.SMEM(block_map.shape, block_map.dtype),
            ints,
            ints,
            pltpu.SemaphoreType.DMA((4,)),
        ],
        name="first",
    )(points, order, compress, block_map)
    received = from_partner(sent, "partner", levels - 1)

    ordered, head, tail = call(
        order_body,
        [jax.ShapeDtypeStruct((leaves, vectors, LANES), jnp.bfloat16), edge, edge],
        [VMEM, VMEM],
        flops=1 << 24,
        name="order",
    )(points, order)
    ends = lax.axis_size("block") - 1
    before = lax.ppermute(tail, "block", [(i, i + 1) for i in range(ends)])
    after = lax.ppermute(head, "block", [(i + 1, i) for i in range(ends)])

    sent = call(
        top_send_body, pair, [SMEM, VMEM, VMEM], [ints] * 4, name="top_send"
    )(block_map, received, top_factor)
    own = call(
        top_own_body, state, [SMEM, VMEM, VMEM, VMEM], [ints] * 2, flops=1 << 24, name="top_own"
    )(block_map, received, top_factor, butterfly_mixers)
    field, place = call(
        near_body,
        [state, jax.ShapeDtypeStruct((8, count), jnp.int32)],
        [SMEM, SMEM, VMEM, VMEM, VMEM, VMEM, VMEM],
        [pltpu.VMEM((leaves + 2 * REACH, vectors, LANES), jnp.bfloat16)],
        flops=1 << 25,
        name="near",
    )(base, neighbours, before, ordered, after, nearby_dense_blocks, order)

    for level in range(1, levels):
        received = from_partner(sent, "partner", levels - 1 - level)
        if level < levels - 1:
            sent = call(
                functools.partial(mix_send_body, level),
                pair,
                [SMEM, VMEM, VMEM, VMEM],
                [ints] * 4,
                name="mix_send",
            )(block_map, received, own, butterfly_mixers)
            own = call(
                functools.partial(mix_own_body, level),
                state,
                [SMEM, VMEM, VMEM, VMEM],
                [ints] * 2,
                flops=1 << 24,
                name="mix_own",
            )(block_map, received, own, butterfly_mixers)
    return call(
        functools.partial(last_body, levels - 1),
        jax.ShapeDtypeStruct(points.shape, points.dtype),
        [SMEM] + [VMEM] * 6,
        [ints] * 2,
        name="last",
    )(block_map, received, own, butterfly_mixers, expand, field, place)


def solution(mesh):
    return jax.shard_map(
        on_device,
        mesh=mesh,
        in_specs=(
            P(None, ("partner", "block")),
            P(("partner", "block")),
            P(("partner", "block"), None, None, None),
            P(("partner", "block"), None),
            P(("partner", "block"), None, None),
            P(("partner", "block"), None, None),
            P(("partner", "block"), None, None),
            P(None, ("partner", "block"), None, None, None),
            P(),
        ),
        out_specs=P(None, ("partner", "block")),
        check_vma=False,
    )
```

time: 37.4 us -> 29.9 us (0.80)
  local copies, waits for them, and re-layouts: 18 us -> 5.38 us
  Pallas kernels: 0 us -> 7.87 us
  matrix products: 2.54 us -> 0 us
  waiting for transfers between devices: 4.2 us -> 5.89 us
  other arithmetic: 0.88 us -> 0 us
  starting transfers between devices: 11.1 us -> 10.3 us
    pallas_call x0 -> x8, Pallas kernels: none -> 7.87 us  [the longest x1 1.83 us: on_device(): call(functools.partial(last_body, levels - 1), jax.ShapeDtypeStruct(point...]
    gather x6 -> x0, local copies, waits for them, and re-layouts: 6.53 us -> none  [the longest x2 3.33 us: on_device(): ordered = jnp.take(points, local_order, axis=1)]
    scatter x2 -> x0, local copies, waits for them, and re-layouts: 3.98 us -> none  [on_device(): return jnp.zeros_like(points).at[:, local_order].set(in_tree)]
    ppermute x2, waiting for transfers between devices: 0.02 us -> 3.56 us  [the longest x1 3.56 us: on_device(): after = lax.ppermute(head, 'block', [(i + 1, i) for i in range(ends)])]
    dot_general x8 -> x0, matrix products: 2.54 us -> none  [the longest x2 0.74 us: mixed_pair(): jnp.einsum('bvk,bkj->bvj', across_partners, widened[:, 1], precision=HI)]
    ppermute x2, starting transfers between devices: 7.49 us -> 5.1 us  [the longest x1 3.81 us: on_device(): before = lax.ppermute(tail, 'block', [(i, i + 1) for i in range(ends)])]
    ppermute x3, waiting for transfers between devices: 4.18 us -> 2.33 us  [from_partner(): lax.ppermute(x, axis, [(i, i ^ 1 << bit) for i in range(lax.axis_size(axi...]
    ppermute x2 -> x0, local copies, waits for them, and re-layouts: 1.8 us -> none  [the longest x1 0.9 us: padded_2(): lax.ppermute(head, axis, [((i + 1) % count, i) for i in range(ends)])]
  transfers between devices with their start and end apart: 5 -> 5, of which waited for: 2 -> 3; matrix products, arithmetic and copies ran while one was open for 13% -> 0% of each run, Pallas kernels for 0% -> 12%
where the time goes in v1:
time: 29.9 us; the launch traced here: 29.5 us
  starting transfers between devices  10.3 us (34%)
  Pallas kernels  7.87 us (26%)
  waiting for transfers between devices  5.89 us (20%)
  local copies, waits for them, and re-layouts  5.38 us (18%)
    unnamed x27, local copies, waits for them, and re-layouts  5.38 us
    ppermute x3, starting transfers between devices, from_partner(): lax.ppermute(x, axis, [(i, i ^ 1 << bit) for i in range(lax.axis_size(axi...  5.19 us
    ppermute x1, starting transfers between devices, on_device(): before = lax.ppermute(tail, 'block', [(i, i + 1) for i in range(ends)])  3.81 us
    ppermute x1, waiting for transfers between devices, on_device(): after = lax.ppermute(head, 'block', [(i + 1, i) for i in range(ends)])  3.56 us
    ppermute x3, waiting for transfers between devices, from_partner(): lax.ppermute(x, axis, [(i, i ^ 1 << bit) for i in range(lax.axis_size(axi...  2.33 us
    pallas_call x1, Pallas kernels, on_device(): call(functools.partial(last_body, levels - 1), jax.ShapeDtypeStruct(point...  1.83 us
    pallas_call x1, Pallas kernels, on_device(): call(near_body, [state, jax.ShapeDtypeStruct((8, count), jnp.int32)], [SM...  1.45 us
    ppermute x1, starting transfers between devices, on_device(): after = lax.ppermute(head, 'block', [(i + 1, i) for i in range(ends)])  1.29 us
  transfers between devices with their start and end apart: 5, of which 3 were waited for; matrix products, arithmetic and copies ran while one was open for 0% of the time, Pallas kernels for 12%

profile of v1, /device:TPU:0, one launch (start us, length us, event | category | flops | bytes accessed | tf_op | source)
XLA Modules:
  0.0 29.5 jit_solution(5920177897894335007)
XLA Ops:
  0.0 0.0 copy-start.2
  0.0 0.0 copy-start.4
  0.0 0.9 %copy-done.4 = bf16[32,1024]{1,0:T(8,128)(2,1)S(1)} copy-done((bf16[32,1024]{1,0:T(8,128)(2,1)S(1)}, bf16[32,1024]{1,0:T(8,128)(2,1)}, u32[]{:S(2)}) %copy-start.4) | copy-done | bytes 65560
  0.9 0.0 copy-start.6
  0.9 0.9 %copy-done.6 = bf16[8,128,128]{2,1,0:T(8,128)(2,1)S(1)} copy-done((bf16[8,128,128]{2,1,0:T(8,128)(2,1)S(1)}, bf16[8,128,128]{2,1,0:T(8,128)(2,1)}, u32[]{:S(2)}) %copy-start.6) | copy-done | bytes 262168
  1.8 0.0 copy-start.8
  1.8 0.7 %copy-done.8 = s32[3,8]{1,0:T(4,128)S(1)} copy-done((s32[3,8]{1,0:T(4,128)S(1)}, s32[3,8]{1,0:T(4,128)}, u32[]{:S(2)}) %copy-start.8) | copy-done | bytes 120
  2.5 0.0 copy-start.10
  2.5 0.7 %copy-done.10 = s32[1024]{0:T(1024)S(1)} copy-done((s32[1024]{0:T(1024)S(1)}, s32[1024]{0:T(1024)}, u32[]{:S(2)}) %copy-start.10) | copy-done | bytes 4120
  3.2 0.0 copy-start.9
  3.2 0.9 %first.1 = bf16[4,64,128]{2,1,0:T(8,128)(2,1)S(1)} custom-call(bf16[32,1024]{1,0:T(8,128)(2,1)S(1)} %copy-done.4, s32[8,128]{1,0:T(8,128)S(1)} %bitcast.2, bf16[8,128,128]{2,1,0:T(8,128)(2,1)S(1)} %copy-done.6, s32[3,8]{1,0:T(4,128)S(1)} %copy-done.8), custom_call_target="tpu_custom_call" | custom-call | flops 1048576 | bytes 262144 | tf_op jit(solution)/shard_map/first/pallas_call | solution.py:209
  4.1 3.1 %collective-permute-start = (bf16[4,64,128]{2,1,0:T(8,128)(2,1)S(1)}, bf16[4,64,128]{2,1,0:T(8,128)(2,1)S(1)}, u32[]{:S(2)}, u32[]{:S(2)}) collective-permute-start(bf16[4,64,128]{2,1,0:T(8,128)(2,1)S(1)} %first.1), channel_id=1, source_target_pairs={{0,16},{4,20},{8,24},{12,28},{16,0},{20,4},{24,8},{28,12},{1,17},{... | collective-permute-start | bytes 196616 | tf_op jit(solution)/shard_map/ppermute | solution.py:183
  7.2 2.2 %collective-permute-done.received = bf16[4,64,128]{2,1,0:T(8,128)(2,1)S(1)} collective-permute-done((bf16[4,64,128]{2,1,0:T(8,128)(2,1)S(1)}, bf16[4,64,128]{2,1,0:T(8,128)(2,1)S(1)}, u32[]{:S(2)}, u32[]{:S(2)}) %collective-permute-start) | collective-permute-done | bytes 65568 | tf_op jit(solution)/shard_map/ppermute | solution.py:183
  9.4 0.0 copy-done.2
  9.4 0.0 copy-done.9
  9.4 0.7 %top_send.1 = bf16[4,64,128]{2,1,0:T(8,128)(2,1)S(1)} custom-call(s32[3,8]{1,0:T(4,128)S(1)} %copy-done.9, bf16[4,64,128]{2,1,0:T(8,128)(2,1)S(1)} %collective-permute-done.received, bf16[8,128,128]{2,1,0:T(8,128)(2,1)S(1)} %copy-done.2), custom_call_target="tpu_custom_call" | custom-call | flops 1048576 | bytes 262144 | tf_op jit(solution)/shard_map/top_send/pallas_call | solution.py:237
  10.2 2.1 %collective-permute-start.1 = (bf16[4,64,128]{2,1,0:T(8,128)(2,1)S(1)}, bf16[4,64,128]{2,1,0:T(8,128)(2,1)S(1)}, u32[]{:S(2)}, u32[]{:S(2)}) collective-permute-start(bf16[4,64,128]{2,1,0:T(8,128)(2,1)S(1)} %top_send.1), channel_id=1, source_target_pairs={{0,8},{4,12},{8,0},{12,4},{16,24},{20,28},{24,16},{28,20},{1,9},{5... | collective-permute-start | bytes 196616 | tf_op jit(solution)/shard_map/ppermute | solution.py:183
  12.3 0.0 copy-start
  12.3 1.2 %copy-done = bf16[2,8,2,128,128]{4,3,2,1,0:T(8,128)(2,1)S(1)} copy-done((bf16[2,8,2,128,128]{4,3,2,1,0:T(8,128)(2,1)S(1)}, bf16[2,8,2,128,128]{4,3,2,1,0:T(8,128)(2,1)}, u32[]{:S(2)}) %copy-start) | copy-done | bytes 1048600
  13.5 0.0 copy-start.1
  13.5 1.0 %top_own.1.own = f32[8,32,128]{2,1,0:T(8,128)S(1)} custom-call(s32[3,8]{1,0:T(4,128)S(1)} %copy-done.9, bf16[4,64,128]{2,1,0:T(8,128)(2,1)S(1)} %collective-permute-done.received, bf16[8,128,128]{2,1,0:T(8,128)(2,1)S(1)} %copy-done.2, bf16[2,8,2,128,128]{4,3,2,1,0:T(8,128)(2,1)S(1)} %copy-done), custom_call_target="tpu_custom_call" | custom-call | flops 16777216 | bytes 262144 | tf_op jit(solution)/shard_map/top_own/pallas_call | solution.py:240
  14.4 0.0 copy-start.5
  14.4 0.0 copy-start.3
  14.4 0.1 collective-permute-done.1.received
  14.5 0.2 copy-done.1
  14.7 0.8 %mix_send.1 = bf16[4,64,128]{2,1,0:T(8,128)(2,1)S(1)} custom-call(s32[3,8]{1,0:T(4,128)S(1)} %copy-done.9, bf16[4,64,128]{2,1,0:T(8,128)(2,1)S(1)} %collective-permute-done.1.received, f32[8,32,128]{2,1,0:T(8,128)S(1)} %top_own.1.own, bf16[2,8,2,128,128]{4,3,2,1,0:T(8,128)(2,1)S(1)} %copy-done.1), custom_call_target="tpu_custom_call" | custom-call | flops 1048576 | bytes 262144 | tf_op jit(solution)/shard_map/mix_send/pallas_call | solution.py:255
  15.5 0.1 collective-permute-start.2
  15.5 0.0 copy-done.5
  15.6 0.2 order.1
  15.8 3.8 %collective-permute-start.3 = (bf16[2,32,128]{2,1,0:T(8,128)(2,1)S(1)}, bf16[2,32,128]{2,1,0:T(8,128)(2,1)S(1)}, u32[]{:S(2)}, u32[]{:S(2)}) collective-permute-start(bf16[2,32,128]{2,1,0:T(8,128)(2,1)S(1)} %get-tuple-element.10), channel_id=1, source_target_pairs={{0,1},{1,2},{2,3},{4,5},{5,6},{6,7},{8,9},{9,10},{10,11},{12,13},{... | collective-permute-start | bytes 49160 | tf_op jit(solution)/shard_map/ppermute | solution.py:234
  19.6 1.3 %collective-permute-start.4 = (bf16[2,32,128]{2,1,0:T(8,128)(2,1)S(1)}, bf16[2,32,128]{2,1,0:T(8,128)(2,1)S(1)}, u32[]{:S(2)}, u32[]{:S(2)}) collective-permute-start(bf16[2,32,128]{2,1,0:T(8,128)(2,1)S(1)} %get-tuple-element.12), channel_id=1, source_target_pairs={{1,0},{2,1},{3,2},{5,4},{6,5},{7,6},{9,8},{10,9},{11,10},{13,12},{... | collective-permute-start | bytes 49160 | tf_op jit(solution)/shard_map/ppermute | solution.py:235
  20.9 0.0 copy-start.12
  20.9 0.7 %copy-done.12 = s32[8,3]{0,1:T(4,128)S(1)} copy-done((s32[8,3]{0,1:T(4,128)S(1)}, s32[8,3]{0,1:T(4,128)}, u32[]{:S(2)}) %copy-start.12) | copy-done | bytes 120
  21.6 0.1 copy.10.near
  21.7 0.0 copy-start.11
  21.7 0.0 collective-permute-done.3.before
  21.7 3.6 %collective-permute-done.4.after = bf16[2,32,128]{2,1,0:T(8,128)(2,1)S(1)} collective-permute-done((bf16[2,32,128]{2,1,0:T(8,128)(2,1)S(1)}, bf16[2,32,128]{2,1,0:T(8,128)(2,1)S(1)}, u32[]{:S(2)}, u32[]{:S(2)}) %collective-permute-start.4) | collective-permute-done | bytes 16416 | tf_op jit(solution)/shard_map/ppermute | solution.py:235
  25.2 0.0 copy-done.3
  25.2 0.0 copy-done.11
  25.2 1.5 %near.2 = (f32[8,32,128]{2,1,0:T(8,128)S(1)}, s32[8,1024]{1,0:T(8,128)S(1)}) custom-call(s32[1]{0:T(128)} %bitcast.1.base, s32[8,3]{1,0:T(8,128)S(1)} %copy.10.near, bf16[2,32,128]{2,1,0:T(8,128)(2,1)S(1)} %collective-permute-done.3.before, bf16[8,32,128]{2,1,0:T(8,128)(2,1)S(1)} %get-tuple-element.11.ordered, ...), custom_call_target="tpu_custom_call" | custom-call | flops 33554432 | bytes 262144 | tf_op jit(solution)/shard_map/near/pallas_call | solution.py:243
  26.7 0.0 copy-start.7
  26.7 1.0 %mix_own.1.own = f32[8,32,128]{2,1,0:T(8,128)S(1)} custom-call(s32[3,8]{1,0:T(4,128)S(1)} %copy-done.9, bf16[4,64,128]{2,1,0:T(8,128)(2,1)S(1)} %collective-permute-done.1.received, f32[8,32,128]{2,1,0:T(8,128)S(1)} %top_own.1.own, bf16[2,8,2,128,128]{4,3,2,1,0:T(8,128)(2,1)S(1)} %copy-done.1), custom_call_target="tpu_custom_call" | custom-call | flops 16777216 | bytes 262144 | tf_op jit(solution)/shard_map/mix_own/pallas_call | solution.py:262
  27.7 0.0 collective-permute-done.2.received
  27.7 0.0 copy-done.7
  27.7 1.8 %last.1 = bf16[32,1024]{1,0:T(8,128)(2,1)} custom-call(s32[3,8]{1,0:T(4,128)S(1)} %copy-done.9, bf16[4,64,128]{2,1,0:T(8,128)(2,1)S(1)} %collective-permute-done.2.received, f32[8,32,128]{2,1,0:T(8,128)S(1)} %mix_own.1.own, bf16[2,8,2,128,128]{4,3,2,1,0:T(8,128)(2,1)S(1)} %copy-done.1, bf16[8,128,128]{2,1,0:T(8,128)(2,1)S(1)} %copy-done.7, ...), custom_call_target="tpu_custom_call" | custom-call | flops 1048576 | bytes 262144 | tf_op jit(solution)/shard_map/last/pallas_call | solution.py:270
Async XLA Ops:
  0.0 9.4 %copy-start.2 = (bf16[8,128,128]{2,1,0:T(8,128)(2,1)S(1)}, bf16[8,128,128]{2,1,0:T(8,128)(2,1)}, u32[]{:S(2)}) copy-start(bf16[8,128,128]{2,1,0:T(8,128)(2,1)} %factor.3) | copy-start | bytes 786436
  0.0 0.9 %copy-start.4 = (bf16[32,1024]{1,0:T(8,128)(2,1)S(1)}, bf16[32,1024]{1,0:T(8,128)(2,1)}, u32[]{:S(2)}) copy-start(bf16[32,1024]{1,0:T(8,128)(2,1)} %points.3) | copy-start | bytes 196612
  0.9 0.9 %copy-start.6 = (bf16[8,128,128]{2,1,0:T(8,128)(2,1)S(1)}, bf16[8,128,128]{2,1,0:T(8,128)(2,1)}, u32[]{:S(2)}) copy-start(bf16[8,128,128]{2,1,0:T(8,128)(2,1)} %compress.1) | copy-start | bytes 786436
  1.8 0.7 %copy-start.8 = (s32[3,8]{1,0:T(4,128)S(1)}, s32[3,8]{1,0:T(4,128)}, u32[]{:S(2)}) copy-start(s32[3,8]{1,0:T(4,128)} %block_map.11) | copy-start | bytes 292
  2.5 0.7 %copy-start.10 = (s32[1024]{0:T(1024)S(1)}, s32[1024]{0:T(1024)}, u32[]{:S(2)}) copy-start(s32[1024]{0:T(1024)} %param.10) | copy-start | bytes 12292
  3.2 6.2 %copy-start.9 = (s32[3,8]{1,0:T(4,128)S(1)}, s32[3,8]{1,0:T(4,128)}, u32[]{:S(2)}) copy-start(s32[3,8]{1,0:T(4,128)} %block_map.11) | copy-start | bytes 292
  4.1 5.3 %collective-permute-start = (bf16[4,64,128]{2,1,0:T(8,128)(2,1)S(1)}, bf16[4,64,128]{2,1,0:T(8,128)(2,1)S(1)}, u32[]{:S(2)}, u32[]{:S(2)}) collective-permute-start(bf16[4,64,128]{2,1,0:T(8,128)(2,1)S(1)} %first.1), channel_id=1, source_target_pairs={{0,16},{4,20},{8,24},{12,28},{16,0},{20,4},{24,8},{28,12},{1,17},{... | collective-permute-start | bytes 196616 | tf_op jit(solution)/shard_map/ppermute | solution.py:183
  10.2 4.3 %collective-permute-start.1 = (bf16[4,64,128]{2,1,0:T(8,128)(2,1)S(1)}, bf16[4,64,128]{2,1,0:T(8,128)(2,1)S(1)}, u32[]{:S(2)}, u32[]{:S(2)}) collective-permute-start(bf16[4,64,128]{2,1,0:T(8,128)(2,1)S(1)} %top_send.1), channel_id=1, source_target_pairs={{0,8},{4,12},{8,0},{12,4},{16,24},{20,28},{24,16},{28,20},{1,9},{5... | collective-permute-start | bytes 196616 | tf_op jit(solution)/shard_map/ppermute | solution.py:183
  12.3 1.2 %copy-start = (bf16[2,8,2,128,128]{4,3,2,1,0:T(8,128)(2,1)S(1)}, bf16[2,8,2,128,128]{4,3,2,1,0:T(8,128)(2,1)}, u32[]{:S(2)}) copy-start(bf16[2,8,2,128,128]{4,3,2,1,0:T(8,128)(2,1)} %mixers.7) | copy-start | bytes 3145732
  13.5 1.2 %copy-start.1 = (bf16[2,8,2,128,128]{4,3,2,1,0:T(8,128)(2,1)S(1)}, bf16[2,8,2,128,128]{4,3,2,1,0:T(8,128)(2,1)}, u32[]{:S(2)}) copy-start(bf16[2,8,2,128,128]{4,3,2,1,0:T(8,128)(2,1)} %mixers.7) | copy-start | bytes 3145732
  14.4 1.1 %copy-start.5 = (bf16[32,1024]{1,0:T(8,128)(2,1)S(1)}, bf16[32,1024]{1,0:T(8,128)(2,1)}, u32[]{:S(2)}) copy-start(bf16[32,1024]{1,0:T(8,128)(2,1)} %points.3) | copy-start | bytes 196612
  14.4 10.8 %copy-start.3 = (bf16[8,3,128,128]{3,2,1,0:T(8,128)(2,1)S(1)}, bf16[8,3,128,128]{3,2,1,0:T(8,128)(2,1)}, u32[]{:S(2)}) copy-start(bf16[8,3,128,128]{3,2,1,0:T(8,128)(2,1)} %blocks.1) | copy-start | bytes 2359300
  15.5 12.2 %collective-permute-start.2 = (bf16[4,64,128]{2,1,0:T(8,128)(2,1)S(1)}, bf16[4,64,128]{2,1,0:T(8,128)(2,1)S(1)}, u32[]{:S(2)}, u32[]{:S(2)}) collective-permute-start(bf16[4,64,128]{2,1,0:T(8,128)(2,1)S(1)} %mix_send.1), channel_id=1, source_target_pairs={{0,4},{4,0},{8,12},{12,8},{16,20},{20,16},{24,28},{28,24},{1,5},{5... | collective-permute-start | bytes 196616 | tf_op jit(solution)/shard_map/ppermute | solution.py:183
  15.8 5.9 %collective-permute-start.3 = (bf16[2,32,128]{2,1,0:T(8,128)(2,1)S(1)}, bf16[2,32,128]{2,1,0:T(8,128)(2,1)S(1)}, u32[]{:S(2)}, u32[]{:S(2)}) collective-permute-start(bf16[2,32,128]{2,1,0:T(8,128)(2,1)S(1)} %get-tuple-element.10), channel_id=1, source_target_pairs={{0,1},{1,2},{2,3},{4,5},{5,6},{6,7},{8,9},{9,10},{10,11},{12,13},{... | collective-permute-start | bytes 49160 | tf_op jit(solution)/shard_map/ppermute | solution.py:234
  19.6 5.6 %collective-permute-start.4 = (bf16[2,32,128]{2,1,0:T(8,128)(2,1)S(1)}, bf16[2,32,128]{2,1,0:T(8,128)(2,1)S(1)}, u32[]{:S(2)}, u32[]{:S(2)}) collective-permute-start(bf16[2,32,128]{2,1,0:T(8,128)(2,1)S(1)} %get-tuple-element.12), channel_id=1, source_target_pairs={{1,0},{2,1},{3,2},{5,4},{6,5},{7,6},{9,8},{10,9},{11,10},{13,12},{... | collective-permute-start | bytes 49160 | tf_op jit(solution)/shard_map/ppermute | solution.py:235
  20.9 0.7 %copy-start.12 = (s32[8,3]{0,1:T(4,128)S(1)}, s32[8,3]{0,1:T(4,128)}, u32[]{:S(2)}) copy-start(s32[8,3]{0,1:T(4,128)} %param.12) | copy-start | bytes 292
  21.7 3.6 %copy-start.11 = (s32[1024]{0:T(1024)S(1)}, s32[1024]{0:T(1024)}, u32[]{:S(2)}) copy-start(s32[1024]{0:T(1024)} %param.10) | copy-start | bytes 12292
  26.7 1.0 %copy-start.7 = (bf16[8,128,128]{2,1,0:T(8,128)(2,1)S(1)}, bf16[8,128,128]{2,1,0:T(8,128)(2,1)}, u32[]{:S(2)}) copy-start(bf16[8,128,128]{2,1,0:T(8,128)(2,1)} %expand.1) | copy-start | bytes 786436

commit v2 on v1

v2 whole, which is shorter than its diff:
```python
import functools

import jax
import jax.numpy as jnp
from jax import lax
from jax.experimental import pallas as pl
from jax.experimental.pallas import tpu as pltpu
from jax.sharding import PartitionSpec as P


REACH = 2
LANES = 128
VMEM = pl.BlockSpec(memory_space=pltpu.VMEM)
HBM = pl.BlockSpec(memory_space=pltpu.HBM)


def call(body, outs, in_specs, scratch=(), flops=1 << 20, moved=1 << 18):
    single = not isinstance(outs, (list, tuple))
    run = pl.pallas_call(
        body,
        out_shape=outs,
        in_specs=in_specs,
        out_specs=VMEM if single else [VMEM] * len(outs),
        scratch_shapes=list(scratch),
        compiler_params=pltpu.CompilerParams(vmem_limit_bytes=16 << 20),
        cost_estimate=pl.CostEstimate(flops=flops, bytes_accessed=moved, transcendentals=0),
    )

    def bound(*args):
        return run(
            *[
                pltpu.with_memory_space_constraint(a, pltpu.HBM) if s is HBM else a
                for a, s in zip(args, in_specs)
            ]
        )

    return bound


def tables(map_ref, row, slot_ref, rank_ref, slots):
    mask = jnp.int32(0)
    for i in range(slots):
        mask = mask | (jnp.int32(1) << map_ref[row, i])
    rank = jnp.int32(0)
    for j in range(slots):
        slot_ref[rank] = jnp.int32(j)
        rank_ref[j] = rank
        rank = rank + ((mask >> j) & 1)


class Places:
    def __init__(self, levels, leaves, near_count):
        self.leaves, self.half = leaves, leaves // 2
        self.level_rows = leaves + 2 * self.half
        self.near_base = levels * self.level_rows
        self.near_count = near_count
        self.rows = -(-(self.near_base + leaves * near_count) // 8) * 8

    def piece(self, level, i):
        return level * self.level_rows + i

    def slot(self, level, k):
        return level * self.level_rows + self.leaves + k

    def slot_piece(self, level, k):
        return level * self.level_rows + self.leaves + self.half + k

    def near(self, leaf, n):
        return self.near_base + leaf * self.near_count + n


def read(table, row):
    return table[pl.ds(row, 1), :][0, 0]


def split(x):
    high = x.astype(jnp.bfloat16)
    low = (x - high.astype(jnp.float32)).astype(jnp.bfloat16)
    return jnp.concatenate([high, low], axis=0)


def times(pair, factor):
    both = jnp.dot(pair, factor, preferred_element_type=jnp.float32)
    rows = both.shape[0] // 2
    return both[:rows] + both[rows:]


def pick_lanes(blocks, high, low):
    rows = blocks[0].shape[0]
    high = jnp.broadcast_to(high, (rows, LANES))
    low = jnp.broadcast_to(low, (rows, LANES))
    out = jnp.take_along_axis(blocks[0], low, axis=1)
    for b in range(1, len(blocks)):
        out = jnp.where(high == b, jnp.take_along_axis(blocks[b], low, axis=1), out)
    return out


def column_blocks(x, leaves):
    return [x[:, b * LANES : (b + 1) * LANES].astype(jnp.float32) for b in range(leaves)]


def first_body(points, order, compress, block_map, sent, pts, idx, comp, table, slot, rank, sems):
    leaves = idx.shape[0]
    copies = [
        pltpu.make_async_copy(block_map, table, sems.at[0]),
        pltpu.make_async_copy(order, idx, sems.at[1]),
        pltpu.make_async_copy(points, pts, sems.at[2]),
        pltpu.make_async_copy(compress, comp, sems.at[3]),
    ]
    for copy in copies:
        copy.start()
    copies[0].wait()
    tables(table, 0, slot, rank, leaves)
    copies[1].wait()
    copies[2].wait()
    blocks = column_blocks(pts[...], leaves)
    rows = []
    for k in range(leaves // 2):
        local = idx[pl.ds(slot[k], 1), :] & (leaves * LANES - 1)
        rows.append(pick_lanes(blocks, local >> 7, local & (LANES - 1)).astype(jnp.bfloat16))
    copies[3].wait()
    for k in range(leaves // 2):
        sent[k] = split(jnp.dot(rows[k], comp[slot[k]], preferred_element_type=jnp.float32))


def order_body(
    places, points, order, block_map, near, ordered, even, odd, table, maps, nears, slot, rank, sems
):
    leaves = order.shape[0]
    levels = maps.shape[0]
    copies = [
        pltpu.make_async_copy(block_map, maps, sems.at[0]),
        pltpu.make_async_copy(near, nears, sems.at[1]),
    ]
    for copy in copies:
        copy.start()
    blocks = column_blocks(points[...], leaves)
    for leaf in range(leaves):
        local = order[pl.ds(leaf, 1), :] & (leaves * LANES - 1)
        ordered[leaf] = pick_lanes(blocks, local >> 7, local & (LANES - 1)).astype(jnp.bfloat16)
    block = lax.axis_index("block")
    parity = block & 1
    head, tail = 0, leaves - REACH
    even[...] = ordered[pl.ds(jnp.where(parity == 0, tail, head), REACH)]
    odd[...] = ordered[pl.ds(jnp.where(parity == 0, head, tail), REACH)]
    base = (lax.axis_index("partner") * lax.axis_size("block") + block) * leaves

    def put(row, value):
        table[pl.ds(row, 1), :] = jnp.full((1, LANES), value, jnp.int32)

    for copy in copies:
        copy.wait()
    for level in range(levels):
        tables(maps, level, slot, rank, leaves)
        for i in range(leaves):
            put(places.piece(level, i), rank[maps[level, i]])
        if level > 0:
            for k in range(leaves // 2):
                i = slot[k]
                put(places.slot(level, k), i)
                put(places.slot_piece(level, k), read(table, places.piece(level - 1, i)))
    for leaf in range(leaves):
        for n in range(nears.shape[0]):
            put(places.near(leaf, n), nears[n, leaf] - base + REACH)


def near_body(places, table, even, ordered, odd, blocks, order, field, place, windows):
    leaves, near_count = blocks.shape[0], blocks.shape[1]
    parity = lax.axis_index("block") & 1
    first, last = 0, leaves + REACH
    windows[pl.ds(jnp.where(parity == 0, last, first), REACH)] = even[...]
    windows[pl.ds(jnp.where(parity == 0, first, last), REACH)] = odd[...]
    windows[pl.ds(REACH, leaves)] = ordered[...]
    for leaf in range(leaves):
        total = None
        for n in range(near_count):
            source = windows[read(table, places.near(leaf, n))]
            term = jnp.dot(source, blocks[leaf, n], preferred_element_type=jnp.float32)
            total = term if total is None else total + term
        field[leaf] = total
    count = leaves * LANES
    target = lax.broadcasted_iota(jnp.int32, (count, LANES), 0)
    kind = lax.broadcasted_iota(jnp.int32, (8, LANES), 0)
    lane = lax.broadcasted_iota(jnp.int32, (8, LANES), 1)
    total = None
    for leaf in range(leaves):
        local = order[pl.ds(leaf, 1), :] & (count - 1)
        hit = jnp.where(target == local, 1.0, 0.0).astype(jnp.bfloat16)
        value = jnp.where(kind == 0, leaf, lane).astype(jnp.float32).astype(jnp.bfloat16)
        term = lax.dot_general(
            value, hit, (((1,), (1,)), ((), ())), preferred_element_type=jnp.float32
        )
        total = term if total is None else total + term
    place[...] = total.astype(jnp.int32)


def top_send_body(places, table, received, factor, sent):
    for k in range(sent.shape[0]):
        i = read(table, places.slot(1, k))
        sent[k] = split(times(received[read(table, places.slot_piece(1, k))], factor[i]))


def top_own_body(places, table, received, factor, mixers, own):
    for i in range(own.shape[0]):
        state = split(times(received[read(table, places.piece(0, i))], factor[i]))
        own[i] = times(state, mixers[0, i, 0])


def mix_send_body(places, level, table, received, own, mixers, sent):
    for k in range(sent.shape[0]):
        i = read(table, places.slot(level + 1, k))
        piece = received[read(table, places.slot_piece(level + 1, k))]
        sent[k] = split(own[i] + times(piece, mixers[level - 1, i, 1]))


def mix_own_body(places, level, table, received, own, mixers, own_next):
    for i in range(own.shape[0]):
        other = times(received[read(table, places.piece(level, i))], mixers[level - 1, i, 1])
        own_next[i] = times(split(own[i] + other), mixers[level, i, 0])


def last_body(places, level, table, received, own, mixers, expand, field, place, applied):
    leaves = own.shape[0]
    blocks = []
    for i in range(leaves):
        other = times(received[read(table, places.piece(level, i))], mixers[level - 1, i, 1])
        far = times(split(own[i] + other), expand[i])
        blocks.append((field[i] + far).astype(jnp.bfloat16).astype(jnp.float32))
    for b in range(leaves):
        high = place[pl.ds(0, 1), b * LANES : (b + 1) * LANES]
        low = place[pl.ds(1, 1), b * LANES : (b + 1) * LANES]
        applied[:, b * LANES : (b + 1) * LANES] = pick_lanes(blocks, high, low).astype(jnp.bfloat16)


def from_partner(x, bit):
    count = lax.axis_size("partner")
    return lax.ppermute(x, "partner", [(i, i ^ 1 << bit) for i in range(count)])


def with_neighbour(x, first):
    count = lax.axis_size("block")
    pairs = [(i, i + 1) for i in range(first, count - 1, 2)]
    return lax.ppermute(x, "block", pairs + [(b, a) for a, b in pairs])


def on_device(
    points,
    tree_order,
    nearby_dense_blocks,
    neighbours,
    compress,
    expand,
    top_factor,
    butterfly_mixers,
    block_map,
):
    vectors, count = points.shape
    leaves, near_count = neighbours.shape
    levels = lax.axis_size("partner").bit_length() - 1
    half = leaves // 2
    places = Places(levels, leaves, near_count)
    order = tree_order.reshape(leaves, LANES)
    ints = pltpu.SMEM((leaves + 1,), jnp.int32)
    pair = jax.ShapeDtypeStruct((half, 2 * vectors, LANES), jnp.bfloat16)
    state = jax.ShapeDtypeStruct((leaves, vectors, LANES), jnp.float32)
    edge = jax.ShapeDtypeStruct((REACH, vectors, LANES), jnp.bfloat16)
    part = functools.partial

    sent = call(
        first_body,
        pair,
        [HBM, HBM, HBM, HBM],
        [
            pltpu.VMEM(points.shape, points.dtype),
            pltpu.VMEM(order.shape, order.dtype),
            pltpu.VMEM(compress.shape, compress.dtype),
            pltpu.SMEM(block_map.shape, block_map.dtype),
            ints,
            ints,
            pltpu.SemaphoreType.DMA((4,)),
        ],
    )(points, order, compress, block_map)
    received = from_partner(sent, levels - 1)

    ordered, even, odd, table = call(
        part(order_body, places),
        [
            jax.ShapeDtypeStruct((leaves, vectors, LANES), jnp.bfloat16),
            edge,
            edge,
            jax.ShapeDtypeStruct((places.rows, LANES), jnp.int32),
        ],
        [VMEM, VMEM, HBM, HBM],
        [
            pltpu.SMEM(block_map.shape, block_map.dtype),
            pltpu.SMEM((near_count, leaves), neighbours.dtype),
            ints,
            ints,
            pltpu.SemaphoreType.DMA((2,)),
        ],
        flops=1 << 24,
    )(points, order, block_map, neighbours.T)
    even = with_neighbour(even, 0)
    odd = with_neighbour(odd, 1)

    sent = call(part(top_send_body, places), pair, [VMEM] * 3)(table, received, top_factor)
    own = call(part(top_own_body, places), state, [VMEM] * 4, flops=1 << 24)(
        table, received, top_factor, butterfly_mixers
    )
    field, place = call(
        part(near_body, places),
        [state, jax.ShapeDtypeStruct((8, count), jnp.int32)],
        [VMEM] * 6,
        [pltpu.VMEM((leaves + 2 * REACH, vectors, LANES), jnp.bfloat16)],
        flops=1 << 25,
    )(table, even, ordered, odd, nearby_dense_blocks, order)

    for level in range(1, levels):
        received = from_partner(sent, levels - 1 - level)
        if level < levels - 1:
            sent = call(part(mix_send_body, places, level), pair, [VMEM] * 4)(
                table, received, own, butterfly_mixers
            )
            own = call(
                part(mix_own_body, places, level), state, [VMEM] * 4, flops=1 << 24
            )(table, received, own, butterfly_mixers)
    return call(
        part(last_body, places, levels - 1),
        jax.ShapeDtypeStruct(points.shape, points.dtype),
        [VMEM] * 7,
    )(table, received, own, butterfly_mixers, expand, field, place)


def solution(mesh):
    return jax.shard_map(
        on_device,
        mesh=mesh,
        in_specs=(
            P(None, ("partner", "block")),
            P(("partner", "block")),
            P(("partner", "block"), None, None, None),
            P(("partner", "block"), None),
            P(("partner", "block"), None, None),
            P(("partner", "block"), None, None),
            P(("partner", "block"), None, None),
            P(None, ("partner", "block"), None, None, None),
            P(),
        ),
        out_specs=P(None, ("partner", "block")),
        check_vma=False,
    )
```

time: 29.9 us -> 21.1 us (0.71)
  the two profiles are of different devices: /device:TPU:0 before, /device:TPU:18 now
where the time goes in v2:
time: 21.1 us; the launch traced here: 20.8 us
  waiting for transfers between devices  7.36 us (35%)
  starting transfers between devices  5.81 us (28%)
  Pallas kernels  5.79 us (27%)
  local copies, waits for them, and re-layouts  1.78 us (8%)
    pallas_call x8, Pallas kernels, bound(): run(*[pltpu.with_memory_space_constraint(a, pltpu.HBM) if s is HBM else a...  5.79 us
    ppermute x2, waiting for transfers between devices, with_neighbour(): return lax.ppermute(x, 'block', pairs + [(b, a) for a, b in pairs])  3.7 us
    ppermute x3, waiting for transfers between devices, from_partner(): return lax.ppermute(x, 'partner', [(i, i ^ 1 << bit) for i in range(count)])  3.66 us
    ppermute x2, starting transfers between devices, with_neighbour(): return lax.ppermute(x, 'block', pairs + [(b, a) for a, b in pairs])  3.55 us
    ppermute x3, starting transfers between devices, from_partner(): return lax.ppermute(x, 'partner', [(i, i ^ 1 << bit) for i in range(count)])  2.26 us
    unnamed x14, local copies, waits for them, and re-layouts  1.78 us
  transfers between devices with their start and end apart: 5, of which 4 were waited for; matrix products, arithmetic and copies ran while one was open for 0% of the time, Pallas kernels for 14%

profile of v2, /device:TPU:18, one launch (start us, length us, event | category | flops | bytes accessed | tf_op | source)
XLA Modules:
  0.0 20.8 jit_solution(18202742903325315211)
XLA Ops:
  0.0 0.0 copy-start.2
  0.0 0.0 copy-start.5
  0.0 0.0 copy-start.6
  0.0 1.3 %shard_map.92 = bf16[4,64,128]{2,1,0:T(8,128)(2,1)S(1)} custom-call(bf16[32,1024]{1,0:T(8,128)(2,1)} %points.3, s32[8,128]{1,0:T(8,128)} %bitcast.2, bf16[8,128,128]{2,1,0:T(8,128)(2,1)} %compress.1, s32[3,8]{1,0:T(4,128)} %block_map.3), custom_call_target="tpu_custom_call" | custom-call | flops 1048576 | bytes 262144 | tf_op jit(solution)/shard_map/pallas_call | solution.py:30
  1.3 1.6 %collective-permute-start = (bf16[4,64,128]{2,1,0:T(8,128)(2,1)S(1)}, bf16[4,64,128]{2,1,0:T(8,128)(2,1)S(1)}, u32[]{:S(2)}, u32[]{:S(2)}) collective-permute-start(bf16[4,64,128]{2,1,0:T(8,128)(2,1)S(1)} %shard_map.92), channel_id=1, source_target_pairs={{0,16},{4,20},{8,24},{12,28},{16,0},{20,4},{24,8},{28,12},{1,17},{... | collective-permute-start | bytes 196616 | tf_op jit(solution)/shard_map/ppermute | solution.py:237
  2.9 0.0 copy-done.5
  2.9 0.0 copy-done.6
  2.9 1.2 %shard_map.91 = (bf16[8,32,128]{2,1,0:T(8,128)(2,1)S(1)}, bf16[2,32,128]{2,1,0:T(8,128)(2,1)S(1)}, bf16[2,32,128]{2,1,0:T(8,128)(2,1)S(1)}, s32[72,128]{1,0:T(8,128)S(1)}) custom-call(bf16[32,1024]{1,0:T(8,128)(2,1)S(1)} %copy-done.5, s32[8,128]{1,0:T(8,128)S(1)} %bitcast.3, s32[3,8]{1,0:T(4,128)} %block_map.3, s32[3,8]{1,0:T(4,128)} %bitcast.5), custom_call_target="tpu_custom_call" | custom-call | flops 16777216 | bytes 262144 | tf_op jit(solution)/shard_map/pallas_call | solution.py:30
  4.0 1.6 %collective-permute-done.received = bf16[4,64,128]{2,1,0:T(8,128)(2,1)S(1)} collective-permute-done((bf16[4,64,128]{2,1,0:T(8,128)(2,1)S(1)}, bf16[4,64,128]{2,1,0:T(8,128)(2,1)S(1)}, u32[]{:S(2)}, u32[]{:S(2)}) %collective-permute-start) | collective-permute-done | bytes 65568 | tf_op jit(solution)/shard_map/ppermute | solution.py:237
  5.6 0.0 copy-done.2
  5.6 0.2 shard_map.93
  5.8 0.6 %collective-permute-start.1 = (bf16[4,64,128]{2,1,0:T(8,128)(2,1)S(1)}, bf16[4,64,128]{2,1,0:T(8,128)(2,1)S(1)}, u32[]{:S(2)}, u32[]{:S(2)}) collective-permute-start(bf16[4,64,128]{2,1,0:T(8,128)(2,1)S(1)} %shard_map.93), channel_id=1, source_target_pairs={{0,8},{4,12},{8,0},{12,4},{16,24},{20,28},{24,16},{28,20},{1,9},{5... | collective-permute-start | bytes 196616 | tf_op jit(solution)/shard_map/ppermute | solution.py:237
  6.4 0.0 copy-start
  6.4 1.2 %copy-done = bf16[2,8,2,128,128]{4,3,2,1,0:T(8,128)(2,1)S(1)} copy-done((bf16[2,8,2,128,128]{4,3,2,1,0:T(8,128)(2,1)S(1)}, bf16[2,8,2,128,128]{4,3,2,1,0:T(8,128)(2,1)}, u32[]{:S(2)}) %copy-start) | copy-done | bytes 1048600
  7.6 0.0 copy-start.1
  7.6 0.4 %shard_map.94.own = f32[8,32,128]{2,1,0:T(8,128)S(1)} custom-call(s32[72,128]{1,0:T(8,128)S(1)} %get-tuple-element.11.table, bf16[4,64,128]{2,1,0:T(8,128)(2,1)S(1)} %collective-permute-done.received, bf16[8,128,128]{2,1,0:T(8,128)(2,1)S(1)} %copy-done.2, bf16[2,8,2,128,128]{4,3,2,1,0:T(8,128)(2,1)S(1)} %copy-done), custom_call_target="tpu_custom_call" | custom-call | flops 16777216 | bytes 262144 | tf_op jit(solution)/shard_map/pallas_call | solution.py:30
  8.0 0.0 copy-start.3
  8.0 2.1 %collective-permute-done.1.received = bf16[4,64,128]{2,1,0:T(8,128)(2,1)S(1)} collective-permute-done((bf16[4,64,128]{2,1,0:T(8,128)(2,1)S(1)}, bf16[4,64,128]{2,1,0:T(8,128)(2,1)S(1)}, u32[]{:S(2)}, u32[]{:S(2)}) %collective-permute-start.1) | collective-permute-done | bytes 65568 | tf_op jit(solution)/shard_map/ppermute | solution.py:237
  10.1 0.0 copy-done.1
  10.1 0.2 shard_map.95
  10.3 0.1 collective-permute-start.2
  10.4 1.6 %collective-permute-start.3 = (bf16[2,32,128]{2,1,0:T(8,128)(2,1)S(1)}, bf16[2,32,128]{2,1,0:T(8,128)(2,1)S(1)}, u32[]{:S(2)}, u32[]{:S(2)}) collective-permute-start(bf16[2,32,128]{2,1,0:T(8,128)(2,1)S(1)} %get-tuple-element.12), channel_id=1, source_target_pairs={{0,1},{2,3},{1,0},{3,2},{4,5},{6,7},{5,4},{7,6},{8,9},{10,11},{9,8... | collective-permute-start | bytes 49160 | tf_op jit(solution)/shard_map/ppermute | solution.py:243
  12.1 1.9 %collective-permute-start.4 = (bf16[2,32,128]{2,1,0:T(8,128)(2,1)S(1)}, bf16[2,32,128]{2,1,0:T(8,128)(2,1)S(1)}, u32[]{:S(2)}, u32[]{:S(2)}) collective-permute-start(bf16[2,32,128]{2,1,0:T(8,128)(2,1)S(1)} %get-tuple-element.14), channel_id=1, source_target_pairs={{1,2},{2,1},{5,6},{6,5},{9,10},{10,9},{13,14},{14,13},{17,18},{18,... | collective-permute-start | bytes 49160 | tf_op jit(solution)/shard_map/ppermute | solution.py:243
  14.0 0.2 %collective-permute-done.3.even = bf16[2,32,128]{2,1,0:T(8,128)(2,1)S(1)} collective-permute-done((bf16[2,32,128]{2,1,0:T(8,128)(2,1)S(1)}, bf16[2,32,128]{2,1,0:T(8,128)(2,1)S(1)}, u32[]{:S(2)}, u32[]{:S(2)}) %collective-permute-start.3) | collective-permute-done | bytes 16416 | tf_op jit(solution)/shard_map/ppermute | solution.py:243
  14.2 3.5 %collective-permute-done.4.odd = bf16[2,32,128]{2,1,0:T(8,128)(2,1)S(1)} collective-permute-done((bf16[2,32,128]{2,1,0:T(8,128)(2,1)S(1)}, bf16[2,32,128]{2,1,0:T(8,128)(2,1)S(1)}, u32[]{:S(2)}, u32[]{:S(2)}) %collective-permute-start.4) | collective-permute-done | bytes 16416 | tf_op jit(solution)/shard_map/ppermute | solution.py:243
  17.7 0.0 copy-done.3
  17.7 0.9 %shard_map.97 = (f32[8,32,128]{2,1,0:T(8,128)S(1)}, s32[8,1024]{1,0:T(8,128)S(1)}) custom-call(s32[72,128]{1,0:T(8,128)S(1)} %get-tuple-element.11.table, bf16[2,32,128]{2,1,0:T(8,128)(2,1)S(1)} %collective-permute-done.3.even, bf16[8,32,128]{2,1,0:T(8,128)(2,1)S(1)} %get-tuple-element.13.ordered, bf16[2,32,128]{2,1,0:T(8,128)(2,1)S(1)} %collective-permute-done.4.odd, ...), custom_call_target="tpu_custom_call" | custom-call | flops 33554432 | bytes 262144 | tf_op jit(solution)/shard_map/pallas_call | solution.py:30
  18.6 0.0 copy-start.4
  18.6 0.4 %shard_map.96.own = f32[8,32,128]{2,1,0:T(8,128)S(1)} custom-call(s32[72,128]{1,0:T(8,128)S(1)} %get-tuple-element.11.table, bf16[4,64,128]{2,1,0:T(8,128)(2,1)S(1)} %collective-permute-done.1.received, f32[8,32,128]{2,1,0:T(8,128)S(1)} %shard_map.94.own, bf16[2,8,2,128,128]{4,3,2,1,0:T(8,128)(2,1)S(1)} %copy-done.1), custom_call_target="tpu_custom_call" | custom-call | flops 16777216 | bytes 262144 | tf_op jit(solution)/shard_map/pallas_call | solution.py:30
  19.0 0.0 collective-permute-done.2.received
  19.0 0.5 %copy-done.4 = bf16[8,128,128]{2,1,0:T(8,128)(2,1)S(1)} copy-done((bf16[8,128,128]{2,1,0:T(8,128)(2,1)S(1)}, bf16[8,128,128]{2,1,0:T(8,128)(2,1)}, u32[]{:S(2)}) %copy-start.4) | copy-done | bytes 262168
  19.5 1.3 %shard_map.98 = bf16[32,1024]{1,0:T(8,128)(2,1)} custom-call(s32[72,128]{1,0:T(8,128)S(1)} %get-tuple-element.11.table, bf16[4,64,128]{2,1,0:T(8,128)(2,1)S(1)} %collective-permute-done.2.received, f32[8,32,128]{2,1,0:T(8,128)S(1)} %shard_map.96.own, bf16[2,8,2,128,128]{4,3,2,1,0:T(8,128)(2,1)S(1)} %copy-done.1, bf16[8,128,128]{2,1,0:T(8,128)(2,1)S(1)} %copy-done.4, ...), custom_call_target="tpu_custom_call" | custom-call | flops 1048576 | bytes 262144 | tf_op jit(solution)/shard_map/pallas_call | solution.py:30
Async XLA Ops:
  0.0 5.6 %copy-start.2 = (bf16[8,128,128]{2,1,0:T(8,128)(2,1)S(1)}, bf16[8,128,128]{2,1,0:T(8,128)(2,1)}, u32[]{:S(2)}) copy-start(bf16[8,128,128]{2,1,0:T(8,128)(2,1)} %factor.3) | copy-start | bytes 786436
  0.0 2.9 %copy-start.5 = (bf16[32,1024]{1,0:T(8,128)(2,1)S(1)}, bf16[32,1024]{1,0:T(8,128)(2,1)}, u32[]{:S(2)}) copy-start(bf16[32,1024]{1,0:T(8,128)(2,1)} %points.3) | copy-start | bytes 196612
  0.0 2.9 %copy-start.6 = (s32[1024]{0:T(1024)S(1)}, s32[1024]{0:T(1024)}, u32[]{:S(2)}) copy-start(s32[1024]{0:T(1024)} %param.10) | copy-start | bytes 12292
  1.3 4.3 %collective-permute-start = (bf16[4,64,128]{2,1,0:T(8,128)(2,1)S(1)}, bf16[4,64,128]{2,1,0:T(8,128)(2,1)S(1)}, u32[]{:S(2)}, u32[]{:S(2)}) collective-permute-start(bf16[4,64,128]{2,1,0:T(8,128)(2,1)S(1)} %shard_map.92), channel_id=1, source_target_pairs={{0,16},{4,20},{8,24},{12,28},{16,0},{20,4},{24,8},{28,12},{1,17},{... | collective-permute-start | bytes 196616 | tf_op jit(solution)/shard_map/ppermute | solution.py:237
  5.8 4.3 %collective-permute-start.1 = (bf16[4,64,128]{2,1,0:T(8,128)(2,1)S(1)}, bf16[4,64,128]{2,1,0:T(8,128)(2,1)S(1)}, u32[]{:S(2)}, u32[]{:S(2)}) collective-permute-start(bf16[4,64,128]{2,1,0:T(8,128)(2,1)S(1)} %shard_map.93), channel_id=1, source_target_pairs={{0,8},{4,12},{8,0},{12,4},{16,24},{20,28},{24,16},{28,20},{1,9},{5... | collective-permute-start | bytes 196616 | tf_op jit(solution)/shard_map/ppermute | solution.py:237
  6.4 1.2 %copy-start = (bf16[2,8,2,128,128]{4,3,2,1,0:T(8,128)(2,1)S(1)}, bf16[2,8,2,128,128]{4,3,2,1,0:T(8,128)(2,1)}, u32[]{:S(2)}) copy-start(bf16[2,8,2,128,128]{4,3,2,1,0:T(8,128)(2,1)} %mixers.7) | copy-start | bytes 3145732
  7.6 2.5 %copy-start.1 = (bf16[2,8,2,128,128]{4,3,2,1,0:T(8,128)(2,1)S(1)}, bf16[2,8,2,128,128]{4,3,2,1,0:T(8,128)(2,1)}, u32[]{:S(2)}) copy-start(bf16[2,8,2,128,128]{4,3,2,1,0:T(8,128)(2,1)} %mixers.7) | copy-start | bytes 3145732
  8.0 9.6 %copy-start.3 = (bf16[8,3,128,128]{3,2,1,0:T(8,128)(2,1)S(1)}, bf16[8,3,128,128]{3,2,1,0:T(8,128)(2,1)}, u32[]{:S(2)}) copy-start(bf16[8,3,128,128]{3,2,1,0:T(8,128)(2,1)} %blocks.1) | copy-start | bytes 2359300
  10.3 8.7 %collective-permute-start.2 = (bf16[4,64,128]{2,1,0:T(8,128)(2,1)S(1)}, bf16[4,64,128]{2,1,0:T(8,128)(2,1)S(1)}, u32[]{:S(2)}, u32[]{:S(2)}) collective-permute-start(bf16[4,64,128]{2,1,0:T(8,128)(2,1)S(1)} %shard_map.95), channel_id=1, source_target_pairs={{0,4},{4,0},{8,12},{12,8},{16,20},{20,16},{24,28},{28,24},{1,5},{5... | collective-permute-start | bytes 196616 | tf_op jit(solution)/shard_map/ppermute | solution.py:237
  10.4 3.8 %collective-permute-start.3 = (bf16[2,32,128]{2,1,0:T(8,128)(2,1)S(1)}, bf16[2,32,128]{2,1,0:T(8,128)(2,1)S(1)}, u32[]{:S(2)}, u32[]{:S(2)}) collective-permute-start(bf16[2,32,128]{2,1,0:T(8,128)(2,1)S(1)} %get-tuple-element.12), channel_id=1, source_target_pairs={{0,1},{2,3},{1,0},{3,2},{4,5},{6,7},{5,4},{7,6},{8,9},{10,11},{9,8... | collective-permute-start | bytes 49160 | tf_op jit(solution)/shard_map/ppermute | solution.py:243
  12.1 5.6 %collective-permute-start.4 = (bf16[2,32,128]{2,1,0:T(8,128)(2,1)S(1)}, bf16[2,32,128]{2,1,0:T(8,128)(2,1)S(1)}, u32[]{:S(2)}, u32[]{:S(2)}) collective-permute-start(bf16[2,32,128]{2,1,0:T(8,128)(2,1)S(1)} %get-tuple-element.14), channel_id=1, source_target_pairs={{1,2},{2,1},{5,6},{6,5},{9,10},{10,9},{13,14},{14,13},{17,18},{18,... | collective-permute-start | bytes 49160 | tf_op jit(solution)/shard_map/ppermute | solution.py:243
  18.6 1.0 %copy-start.4 = (bf16[8,128,128]{2,1,0:T(8,128)(2,1)S(1)}, bf16[8,128,128]{2,1,0:T(8,128)(2,1)}, u32[]{:S(2)}) copy-start(bf16[8,128,128]{2,1,0:T(8,128)(2,1)} %expand.1) | copy-start | bytes 786436

commit v3 on v2

--- a/solution.py
+++ b/solution.py
@@ -14,13 +14,13 @@
 HBM = pl.BlockSpec(memory_space=pltpu.HBM)
 
 
-def call(body, outs, in_specs, scratch=(), flops=1 << 20, moved=1 << 18):
+def call(body, outs, in_specs, scratch=(), flops=1 << 20, moved=1 << 18, place=VMEM):
     single = not isinstance(outs, (list, tuple))
     run = pl.pallas_call(
         body,
         out_shape=outs,
         in_specs=in_specs,
-        out_specs=VMEM if single else [VMEM] * len(outs),
+        out_specs=place if single else [VMEM] * len(outs),
         scratch_shapes=list(scratch),
         compiler_params=pltpu.CompilerParams(vmem_limit_bytes=16 << 20),
         cost_estimate=pl.CostEstimate(flops=flops, bytes_accessed=moved, transcendentals=0),
@@ -124,13 +124,16 @@
 
 
 def order_body(
-    places, points, order, block_map, near, ordered, even, odd, table, maps, nears, slot, rank, sems
+    places, points, order, block_map, near, mixers, dense,
+    ordered, even, odd, table, mixers_out, dense_out, maps, nears, slot, rank, sems,
 ):
     leaves = order.shape[0]
     levels = maps.shape[0]
     copies = [
         pltpu.make_async_copy(block_map, maps, sems.at[0]),
         pltpu.make_async_copy(near, nears, sems.at[1]),
+        pltpu.make_async_copy(mixers, mixers_out, sems.at[2]),
+        pltpu.make_async_copy(dense, dense_out, sems.at[3]),
     ]
     for copy in copies:
         copy.start()
@@ -148,8 +151,8 @@
     def put(row, value):
         table[pl.ds(row, 1), :] = jnp.full((1, LANES), value, jnp.int32)
 
-    for copy in copies:
-        copy.wait()
+    copies[0].wait()
+    copies[1].wait()
     for level in range(levels):
         tables(maps, level, slot, rank, leaves)
         for i in range(leaves):
@@ -162,9 +165,13 @@
     for leaf in range(leaves):
         for n in range(nears.shape[0]):
             put(places.near(leaf, n), nears[n, leaf] - base + REACH)
-
-
-def near_body(places, table, even, ordered, odd, blocks, order, field, place, windows):
+    copies[2].wait()
+    copies[3].wait()
+
+
+def near_body(
+    places, table, even, ordered, odd, blocks, order, mixers, expand, field, place, joint, windows
+):
     leaves, near_count = blocks.shape[0], blocks.shape[1]
     parity = lax.axis_index("block") & 1
     first, last = 0, leaves + REACH
@@ -192,6 +199,11 @@
         )
         total = term if total is None else total + term
     place[...] = total.astype(jnp.int32)
+    for i in range(leaves):
+        both = jnp.dot(mixers[mixers.shape[0] - 1, i, 1], expand[i], preferred_element_type=jnp.float32)
+        high = both.astype(jnp.bfloat16)
+        joint[i, :, :LANES] = high
+        joint[i, :, LANES:] = (both - high.astype(jnp.float32)).astype(jnp.bfloat16)
 
 
 def top_send_body(places, table, received, factor, sent):
@@ -219,17 +231,38 @@
         own_next[i] = times(split(own[i] + other), mixers[level, i, 0])
 
 
-def last_body(places, level, table, received, own, mixers, expand, field, place, applied):
-    leaves = own.shape[0]
+def base_body(places, level, table, received, own, mixers, expand, field, base):
+    for i in range(own.shape[0]):
+        if level:
+            other = times(received[read(table, places.piece(level, i))], mixers[level - 1, i, 1])
+            state = times(split(own[i] + other), mixers[level, i, 0])
+        else:
+            state = own[i]
+        base[i] = field[i] + times(split(state), expand[i])
+
+
+def last_body(places, level, table, received, base, joint, place, applied, rows, sems):
+    leaves = base.shape[0]
     blocks = []
     for i in range(leaves):
-        other = times(received[read(table, places.piece(level, i))], mixers[level - 1, i, 1])
-        far = times(split(own[i] + other), expand[i])
-        blocks.append((field[i] + far).astype(jnp.bfloat16).astype(jnp.float32))
-    for b in range(leaves):
-        high = place[pl.ds(0, 1), b * LANES : (b + 1) * LANES]
-        low = place[pl.ds(1, 1), b * LANES : (b + 1) * LANES]
-        applied[:, b * LANES : (b + 1) * LANES] = pick_lanes(blocks, high, low).astype(jnp.bfloat16)
+        piece = received[read(table, places.piece(level, i))]
+        far = jnp.dot(piece, joint[i], preferred_element_type=jnp.float32)
+        half = far.shape[0] // 2
+        far = (far[:half, :LANES] + far[half:, :LANES]) + (far[:half, LANES:] + far[half:, LANES:])
+        blocks.append((base[i] + far).astype(jnp.bfloat16).astype(jnp.float32))
+    group = rows.shape[0] // sems.shape[0]
+    copies = []
+    for g in range(sems.shape[0]):
+        here = slice(g * group, (g + 1) * group)
+        part = [block[here] for block in blocks]
+        for b in range(leaves):
+            lanes = slice(b * LANES, (b + 1) * LANES)
+            picked = pick_lanes(part, place[pl.ds(0, 1), lanes], place[pl.ds(1, 1), lanes])
+            rows[here, lanes] = picked.astype(jnp.bfloat16)
+        copies.append(pltpu.make_async_copy(rows.at[here], applied.at[here], sems.at[g]))
+        copies[-1].start()
+    for copy in copies:
+        copy.wait()
 
 
 def from_partner(x, bit):
@@ -239,8 +272,10 @@
 
 def with_neighbour(x, first):
     count = lax.axis_size("block")
-    pairs = [(i, i + 1) for i in range(first, count - 1, 2)]
-    return lax.ppermute(x, "block", pairs + [(b, a) for a, b in pairs])
+    to = list(range(count))
+    for i in range(first, count - 1, 2):
+        to[i], to[i + 1] = i + 1, i
+    return lax.ppermute(x, "block", list(enumerate(to)))
 
 
 def on_device(
@@ -282,53 +317,69 @@
     )(points, order, compress, block_map)
     received = from_partner(sent, levels - 1)
 
-    ordered, even, odd, table = call(
+    ordered, even, odd, table, mixers, dense = call(
         part(order_body, places),
         [
             jax.ShapeDtypeStruct((leaves, vectors, LANES), jnp.bfloat16),
             edge,
             edge,
             jax.ShapeDtypeStruct((places.rows, LANES), jnp.int32),
+            jax.ShapeDtypeStruct(butterfly_mixers.shape, butterfly_mixers.dtype),
+            jax.ShapeDtypeStruct(nearby_dense_blocks.shape, nearby_dense_blocks.dtype),
         ],
-        [VMEM, VMEM, HBM, HBM],
+        [VMEM, VMEM, HBM, HBM, HBM, HBM],
         [
             pltpu.SMEM(block_map.shape, block_map.dtype),
             pltpu.SMEM((near_count, leaves), neighbours.dtype),
             ints,
             ints,
-            pltpu.SemaphoreType.DMA((2,)),
+            pltpu.SemaphoreType.DMA((4,)),
         ],
         flops=1 << 24,
-    )(points, order, block_map, neighbours.T)
+    )(points, order, block_map, neighbours.T, butterfly_mixers, nearby_dense_blocks)
     even = with_neighbour(even, 0)
     odd = with_neighbour(odd, 1)
 
     sent = call(part(top_send_body, places), pair, [VMEM] * 3)(table, received, top_factor)
     own = call(part(top_own_body, places), state, [VMEM] * 4, flops=1 << 24)(
-        table, received, top_factor, butterfly_mixers
+        table, received, top_factor, mixers
     )
-    field, place = call(
+    field, place, joint = call(
         part(near_body, places),
-        [state, jax.ShapeDtypeStruct((8, count), jnp.int32)],
-        [VMEM] * 6,
+        [
+            state,
+            jax.ShapeDtypeStruct((8, count), jnp.int32),
+            jax.ShapeDtypeStruct((leaves, LANES, 2 * LANES), jnp.bfloat16),
+        ],
+        [VMEM] * 8,
         [pltpu.VMEM((leaves + 2 * REACH, vectors, LANES), jnp.bfloat16)],
         flops=1 << 25,
-    )(table, even, ordered, odd, nearby_dense_blocks, order)
+    )(table, even, ordered, odd, dense, order, mixers, expand)
 
     for level in range(1, levels):
         received = from_partner(sent, levels - 1 - level)
         if level < levels - 1:
             sent = call(part(mix_send_body, places, level), pair, [VMEM] * 4)(
-                table, received, own, butterfly_mixers
+                table, received, own, mixers
             )
-            own = call(
-                part(mix_own_body, places, level), state, [VMEM] * 4, flops=1 << 24
-            )(table, received, own, butterfly_mixers)
+            if level < levels - 2:
+                own = call(
+                    part(mix_own_body, places, level), state, [VMEM] * 4, flops=1 << 24
+                )(table, received, own, mixers)
+        if level == max(levels - 2, 1):
+            base = call(
+                part(base_body, places, level if levels > 2 else 0),
+                state,
+                [VMEM] * 6,
+                flops=1 << 24,
+            )(table, received, own, mixers, expand, field)
     return call(
         part(last_body, places, levels - 1),
         jax.ShapeDtypeStruct(points.shape, points.dtype),
-        [VMEM] * 7,
-    )(table, received, own, butterfly_mixers, expand, field, place)
+        [VMEM] * 5,
+        [pltpu.VMEM(points.shape, points.dtype), pltpu.SemaphoreType.DMA((4,))],
+        place=HBM,
+    )(table, received, base, joint, place)
 
 
 def solution(mesh):

time: 21.1 us -> 21.5 us (1.019)
  the two profiles are of different devices: /device:TPU:18 before, /device:TPU:16 now
where the time goes in v3:
time: 21.5 us; the launch traced here: 21.4 us
  Pallas kernels  7.3 us (34%)
  waiting for transfers between devices  7.2 us (33%)
  starting transfers between devices  6.76 us (31%)
    pallas_call x8, Pallas kernels, bound(): run(*[pltpu.with_memory_space_constraint(a, pltpu.HBM) if s is HBM else a...  7.3 us
    ppermute x2, waiting for transfers between devices, with_neighbour(): return lax.ppermute(x, 'block', list(enumerate(to)))  3.7 us
    ppermute x2, starting transfers between devices, with_neighbour(): return lax.ppermute(x, 'block', list(enumerate(to)))  3.55 us
    ppermute x3, waiting for transfers between devices, from_partner(): return lax.ppermute(x, 'partner', [(i, i ^ 1 << bit) for i in range(count)])  3.5 us
    ppermute x3, starting transfers between devices, from_partner(): return lax.ppermute(x, 'partner', [(i, i ^ 1 << bit) for i in range(count)])  3.21 us
  transfers between devices with their start and end apart: 5, of which 4 were waited for; matrix products, arithmetic and copies ran while one was open for 0% of the time, Pallas kernels for 21%

profile of v3, /device:TPU:16, one launch (start us, length us, event | category | flops | bytes accessed | tf_op | source)
XLA Modules:
  0.0 21.4 jit_solution(6956299103481429621)
XLA Ops:
  0.0 0.0 copy-start.2
  0.0 0.0 copy-start.3
  0.0 1.3 %shard_map.92 = bf16[4,64,128]{2,1,0:T(8,128)(2,1)S(1)} custom-call(bf16[32,1024]{1,0:T(8,128)(2,1)} %points.3, s32[8,128]{1,0:T(8,128)} %bitcast.2, bf16[8,128,128]{2,1,0:T(8,128)(2,1)} %compress.1, s32[3,8]{1,0:T(4,128)} %block_map.3), custom_call_target="tpu_custom_call" | custom-call | flops 1048576 | bytes 262144 | tf_op jit(solution)/shard_map/pallas_call | solution.py:30
  1.3 1.6 %collective-permute-start = (bf16[4,64,128]{2,1,0:T(8,128)(2,1)S(1)}, bf16[4,64,128]{2,1,0:T(8,128)(2,1)S(1)}, u32[]{:S(2)}, u32[]{:S(2)}) collective-permute-start(bf16[4,64,128]{2,1,0:T(8,128)(2,1)S(1)} %shard_map.92), channel_id=1, source_target_pairs={{0,16},{4,20},{8,24},{12,28},{16,0},{20,4},{24,8},{28,12},{1,17},{... | collective-permute-start | bytes 196616 | tf_op jit(solution)/shard_map/ppermute | solution.py:270
  2.9 0.0 copy-done.2
  2.9 0.0 copy-done.3
  2.9 0.0 copy-start.1
  2.9 1.6 %shard_map.91 = (bf16[8,32,128]{2,1,0:T(8,128)(2,1)S(1)}, bf16[2,32,128]{2,1,0:T(8,128)(2,1)S(1)}, bf16[2,32,128]{2,1,0:T(8,128)(2,1)S(1)}, s32[72,128]{1,0:T(8,...) custom-call(bf16[32,1024]{1,0:T(8,128)(2,1)S(1)} %copy-done.2, ...), custom_call_target="tpu_custom_call" | custom-call | flops 16777216 | bytes 262144 | tf_op jit(solution)/shard_map/pallas_call | solution.py:30
  4.5 1.1 %collective-permute-done.received = bf16[4,64,128]{2,1,0:T(8,128)(2,1)S(1)} collective-permute-done((bf16[4,64,128]{2,1,0:T(8,128)(2,1)S(1)}, bf16[4,64,128]{2,1,0:T(8,128)(2,1)S(1)}, u32[]{:S(2)}, u32[]{:S(2)}) %collective-permute-start) | collective-permute-done | bytes 65568 | tf_op jit(solution)/shard_map/ppermute | solution.py:270
  5.6 0.0 copy-done.1
  5.6 0.2 shard_map.93
  5.8 1.6 %collective-permute-start.1 = (bf16[4,64,128]{2,1,0:T(8,128)(2,1)S(1)}, bf16[4,64,128]{2,1,0:T(8,128)(2,1)S(1)}, u32[]{:S(2)}, u32[]{:S(2)}) collective-permute-start(bf16[4,64,128]{2,1,0:T(8,128)(2,1)S(1)} %shard_map.93), channel_id=1, source_target_pairs={{0,8},{4,12},{8,0},{12,4},{16,24},{20,28},{24,16},{28,20},{1,9},{5... | collective-permute-start | bytes 196616 | tf_op jit(solution)/shard_map/ppermute | solution.py:270
  7.4 0.4 %shard_map.94.own = f32[8,32,128]{2,1,0:T(8,128)S(1)} custom-call(s32[72,128]{1,0:T(8,128)S(1)} %get-tuple-element.14.table, bf16[4,64,128]{2,1,0:T(8,128)(2,1)S(1)} %collective-permute-done.received, bf16[8,128,128]{2,1,0:T(8,128)(2,1)S(1)} %copy-done.1, bf16[2,8,2,128,128]{4,3,2,1,0:T(8,128)(2,1)S(1)} %get-tuple-element.15.mixers), custom_call_target="tpu_custom_call" | custom-call | flops 16777216 | bytes 262144 | tf_op jit(solution)/shard_map/pallas_call | solution.py:30
  7.8 0.0 copy-start
  7.8 2.4 %collective-permute-done.1.received = bf16[4,64,128]{2,1,0:T(8,128)(2,1)S(1)} collective-permute-done((bf16[4,64,128]{2,1,0:T(8,128)(2,1)S(1)}, bf16[4,64,128]{2,1,0:T(8,128)(2,1)S(1)}, u32[]{:S(2)}, u32[]{:S(2)}) %collective-permute-start.1) | collective-permute-done | bytes 65568 | tf_op jit(solution)/shard_map/ppermute | solution.py:270
  10.1 0.2 shard_map.95
  10.3 0.1 collective-permute-start.2
  10.4 1.6 %collective-permute-start.3 = (bf16[2,32,128]{2,1,0:T(8,128)(2,1)S(1)}, bf16[2,32,128]{2,1,0:T(8,128)(2,1)S(1)}, u32[]{:S(2)}, u32[]{:S(2)}) collective-permute-start(bf16[2,32,128]{2,1,0:T(8,128)(2,1)S(1)} %get-tuple-element.16), channel_id=1, source_target_pairs={{0,1},{1,0},{2,3},{3,2},{4,5},{5,4},{6,7},{7,6},{8,9},{9,8},{10,11... | collective-permute-start | bytes 49160 | tf_op jit(solution)/shard_map/ppermute | solution.py:278
  12.1 1.9 %collective-permute-start.4 = (bf16[2,32,128]{2,1,0:T(8,128)(2,1)S(1)}, bf16[2,32,128]{2,1,0:T(8,128)(2,1)S(1)}, u32[]{:S(2)}, u32[]{:S(2)}) collective-permute-start(bf16[2,32,128]{2,1,0:T(8,128)(2,1)S(1)} %get-tuple-element.18), channel_id=1, source_target_pairs={{0,0},{1,2},{2,1},{3,3},{4,4},{5,6},{6,5},{7,7},{8,8},{9,10},{10,9... | collective-permute-start | bytes 49160 | tf_op jit(solution)/shard_map/ppermute | solution.py:278
  14.0 0.2 %collective-permute-done.3.even = bf16[2,32,128]{2,1,0:T(8,128)(2,1)S(1)} collective-permute-done((bf16[2,32,128]{2,1,0:T(8,128)(2,1)S(1)}, bf16[2,32,128]{2,1,0:T(8,128)(2,1)S(1)}, u32[]{:S(2)}, u32[]{:S(2)}) %collective-permute-start.3) | collective-permute-done | bytes 16416 | tf_op jit(solution)/shard_map/ppermute | solution.py:278
  14.2 3.5 %collective-permute-done.4.odd = bf16[2,32,128]{2,1,0:T(8,128)(2,1)S(1)} collective-permute-done((bf16[2,32,128]{2,1,0:T(8,128)(2,1)S(1)}, bf16[2,32,128]{2,1,0:T(8,128)(2,1)S(1)}, u32[]{:S(2)}, u32[]{:S(2)}) %collective-permute-start.4) | collective-permute-done | bytes 16416 | tf_op jit(solution)/shard_map/ppermute | solution.py:278
  17.7 0.0 copy-done
  17.7 1.0 %shard_map.96 = (f32[8,32,128]{2,1,0:T(8,128)S(1)}, s32[8,1024]{1,0:T(8,128)S(1)}, bf16[8,128,256]{2,1,0:T(8,128)(2,1)S(1)}) custom-call(s32[72,128]{1,0:T(8,128)S(1)} %get-tuple-element.14.table, bf16[2,32,128]{2,1,0:T(8,128)(2,1)S(1)} %collective-permute-done.3.even, bf16[8,32,128]{2,1,0:T(8,128)(2,1)S(1)} %get-tuple-element.17.ordered, ...), custom_call_target="tpu_custom_call" | custom-call | flops 33554432 | bytes 262144 | tf_op jit(solution)/shard_map/pallas_call | solution.py:30
  18.7 1.4 %shard_map.97.base = f32[8,32,128]{2,1,0:T(8,128)S(1)} custom-call(s32[72,128]{1,0:T(8,128)S(1)} %get-tuple-element.14.table, bf16[4,64,128]{2,1,0:T(8,128)(2,1)S(1)} %collective-permute-done.1.received, f32[8,32,128]{2,1,0:T(8,128)S(1)} %shard_map.94.own, bf16[2,8,2,128,128]{4,3,2,1,0:T(8,128)(2,1)S(1)} %get-tuple-element.15.mixers, ...), custom_call_target="tpu_custom_call" | custom-call | flops 16777216 | bytes 262144 | tf_op jit(solution)/shard_map/pallas_call | solution.py:30
  20.1 0.0 collective-permute-done.2.received
  20.1 1.2 %shard_map.98 = bf16[32,1024]{1,0:T(8,128)(2,1)} custom-call(s32[72,128]{1,0:T(8,128)S(1)} %get-tuple-element.14.table, bf16[4,64,128]{2,1,0:T(8,128)(2,1)S(1)} %collective-permute-done.2.received, f32[8,32,128]{2,1,0:T(8,128)S(1)} %shard_map.97.base, bf16[8,128,256]{2,1,0:T(8,128)(2,1)S(1)} %get-tuple-element.21.joint, s32[8,1024]{1,0:T(8,128)S(1)} %get-tuple-element.22.place), custom_call_target="tpu_custom_call" | custom-call | flops 1048576 | bytes 262144 | tf_op jit(solution)/shard_map/pallas_call | solution.py:30
Async XLA Ops:
  0.0 2.9 %copy-start.2 = (bf16[32,1024]{1,0:T(8,128)(2,1)S(1)}, bf16[32,1024]{1,0:T(8,128)(2,1)}, u32[]{:S(2)}) copy-start(bf16[32,1024]{1,0:T(8,128)(2,1)} %points.3) | copy-start | bytes 196612
  0.0 2.9 %copy-start.3 = (s32[1024]{0:T(1024)S(1)}, s32[1024]{0:T(1024)}, u32[]{:S(2)}) copy-start(s32[1024]{0:T(1024)} %param.10) | copy-start | bytes 12292
  1.3 4.3 %collective-permute-start = (bf16[4,64,128]{2,1,0:T(8,128)(2,1)S(1)}, bf16[4,64,128]{2,1,0:T(8,128)(2,1)S(1)}, u32[]{:S(2)}, u32[]{:S(2)}) collective-permute-start(bf16[4,64,128]{2,1,0:T(8,128)(2,1)S(1)} %shard_map.92), channel_id=1, source_target_pairs={{0,16},{4,20},{8,24},{12,28},{16,0},{20,4},{24,8},{28,12},{1,17},{... | collective-permute-start | bytes 196616 | tf_op jit(solution)/shard_map/ppermute | solution.py:270
  2.9 2.7 %copy-start.1 = (bf16[8,128,128]{2,1,0:T(8,128)(2,1)S(1)}, bf16[8,128,128]{2,1,0:T(8,128)(2,1)}, u32[]{:S(2)}) copy-start(bf16[8,128,128]{2,1,0:T(8,128)(2,1)} %factor.3) | copy-start | bytes 786436
  5.8 4.3 %collective-permute-start.1 = (bf16[4,64,128]{2,1,0:T(8,128)(2,1)S(1)}, bf16[4,64,128]{2,1,0:T(8,128)(2,1)S(1)}, u32[]{:S(2)}, u32[]{:S(2)}) collective-permute-start(bf16[4,64,128]{2,1,0:T(8,128)(2,1)S(1)} %shard_map.93), channel_id=1, source_target_pairs={{0,8},{4,12},{8,0},{12,4},{16,24},{20,28},{24,16},{28,20},{1,9},{5... | collective-permute-start | bytes 196616 | tf_op jit(solution)/shard_map/ppermute | solution.py:270
  7.8 9.9 %copy-start = (bf16[8,128,128]{2,1,0:T(8,128)(2,1)S(1)}, bf16[8,128,128]{2,1,0:T(8,128)(2,1)}, u32[]{:S(2)}) copy-start(bf16[8,128,128]{2,1,0:T(8,128)(2,1)} %expand.3) | copy-start | bytes 786436
  10.3 9.8 %collective-permute-start.2 = (bf16[4,64,128]{2,1,0:T(8,128)(2,1)S(1)}, bf16[4,64,128]{2,1,0:T(8,128)(2,1)S(1)}, u32[]{:S(2)}, u32[]{:S(2)}) collective-permute-start(bf16[4,64,128]{2,1,0:T(8,128)(2,1)S(1)} %shard_map.95), channel_id=1, source_target_pairs={{0,4},{4,0},{8,12},{12,8},{16,20},{20,16},{24,28},{28,24},{1,5},{5... | collective-permute-start | bytes 196616 | tf_op jit(solution)/shard_map/ppermute | solution.py:270
  10.4 3.8 %collective-permute-start.3 = (bf16[2,32,128]{2,1,0:T(8,128)(2,1)S(1)}, bf16[2,32,128]{2,1,0:T(8,128)(2,1)S(1)}, u32[]{:S(2)}, u32[]{:S(2)}) collective-permute-start(bf16[2,32,128]{2,1,0:T(8,128)(2,1)S(1)} %get-tuple-element.16), channel_id=1, source_target_pairs={{0,1},{1,0},{2,3},{3,2},{4,5},{5,4},{6,7},{7,6},{8,9},{9,8},{10,11... | collective-permute-start | bytes 49160 | tf_op jit(solution)/shard_map/ppermute | solution.py:278
  12.1 5.6 %collective-permute-start.4 = (bf16[2,32,128]{2,1,0:T(8,128)(2,1)S(1)}, bf16[2,32,128]{2,1,0:T(8,128)(2,1)S(1)}, u32[]{:S(2)}, u32[]{:S(2)}) collective-permute-start(bf16[2,32,128]{2,1,0:T(8,128)(2,1)S(1)} %get-tuple-element.18), channel_id=1, source_target_pairs={{0,0},{1,2},{2,1},{3,3},{4,4},{5,6},{6,5},{7,7},{8,8},{9,10},{10,9... | collective-permute-start | bytes 49160 | tf_op jit(solution)/shard_map/ppermute | solution.py:278

commit v4 on v3

--- a/solution.py
+++ b/solution.py
@@ -124,8 +124,8 @@
 
 
 def order_body(
-    places, points, order, block_map, near, mixers, dense,
-    ordered, even, odd, table, mixers_out, dense_out, maps, nears, slot, rank, sems,
+    places, points, order, block_map, near, mixers, dense, expand,
+    ordered, even, odd, table, mixers_out, dense_out, expand_out, maps, nears, slot, rank, sems,
 ):
     leaves = order.shape[0]
     levels = maps.shape[0]
@@ -134,6 +134,7 @@
         pltpu.make_async_copy(near, nears, sems.at[1]),
         pltpu.make_async_copy(mixers, mixers_out, sems.at[2]),
         pltpu.make_async_copy(dense, dense_out, sems.at[3]),
+        pltpu.make_async_copy(expand, expand_out, sems.at[4]),
     ]
     for copy in copies:
         copy.start()
@@ -165,12 +166,12 @@
     for leaf in range(leaves):
         for n in range(nears.shape[0]):
             put(places.near(leaf, n), nears[n, leaf] - base + REACH)
-    copies[2].wait()
-    copies[3].wait()
+    for copy in copies[2:]:
+        copy.wait()
 
 
 def near_body(
-    places, table, even, ordered, odd, blocks, order, mixers, expand, field, place, joint, windows
+    places, table, even, ordered, odd, blocks, order, mixers, expand, field, place, joint_own, joint, windows
 ):
     leaves, near_count = blocks.shape[0], blocks.shape[1]
     parity = lax.axis_index("block") & 1
@@ -199,11 +200,14 @@
         )
         total = term if total is None else total + term
     place[...] = total.astype(jnp.int32)
-    for i in range(leaves):
-        both = jnp.dot(mixers[mixers.shape[0] - 1, i, 1], expand[i], preferred_element_type=jnp.float32)
-        high = both.astype(jnp.bfloat16)
-        joint[i, :, :LANES] = high
-        joint[i, :, LANES:] = (both - high.astype(jnp.float32)).astype(jnp.bfloat16)
+    for side, out in enumerate((joint_own, joint)):
+        for i in range(leaves):
+            both = jnp.dot(
+                mixers[mixers.shape[0] - 1, i, side], expand[i], preferred_element_type=jnp.float32
+            )
+            high = both.astype(jnp.bfloat16)
+            out[i, :, :LANES] = high
+            out[i, :, LANES:] = (both - high.astype(jnp.float32)).astype(jnp.bfloat16)
 
 
 def top_send_body(places, table, received, factor, sent):
@@ -231,14 +235,16 @@
         own_next[i] = times(split(own[i] + other), mixers[level, i, 0])
 
 
-def base_body(places, level, table, received, own, mixers, expand, field, base):
+def times_joint(pair, joint):
+    both = jnp.dot(pair, joint, preferred_element_type=jnp.float32)
+    rows = both.shape[0] // 2
+    return (both[:rows, :LANES] + both[rows:, :LANES]) + (both[:rows, LANES:] + both[rows:, LANES:])
+
+
+def base_body(places, level, table, received, own, mixers, joint_own, field, base):
     for i in range(own.shape[0]):
-        if level:
-            other = times(received[read(table, places.piece(level, i))], mixers[level - 1, i, 1])
-            state = times(split(own[i] + other), mixers[level, i, 0])
-        else:
-            state = own[i]
-        base[i] = field[i] + times(split(state), expand[i])
+        other = times(received[read(table, places.piece(level, i))], mixers[level - 1, i, 1])
+        base[i] = field[i] + times_joint(split(own[i] + other), joint_own[i])
 
 
 def last_body(places, level, table, received, base, joint, place, applied, rows, sems):
@@ -246,10 +252,7 @@
     blocks = []
     for i in range(leaves):
         piece = received[read(table, places.piece(level, i))]
-        far = jnp.dot(piece, joint[i], preferred_element_type=jnp.float32)
-        half = far.shape[0] // 2
-        far = (far[:half, :LANES] + far[half:, :LANES]) + (far[:half, LANES:] + far[half:, LANES:])
-        blocks.append((base[i] + far).astype(jnp.bfloat16).astype(jnp.float32))
+        blocks.append((base[i] + times_joint(piece, joint[i])).astype(jnp.bfloat16).astype(jnp.float32))
     group = rows.shape[0] // sems.shape[0]
     copies = []
     for g in range(sems.shape[0]):
@@ -271,11 +274,14 @@
 
 
 def with_neighbour(x, first):
-    count = lax.axis_size("block")
-    to = list(range(count))
-    for i in range(first, count - 1, 2):
-        to[i], to[i + 1] = i + 1, i
-    return lax.ppermute(x, "block", list(enumerate(to)))
+    groups, count = lax.axis_size("partner"), lax.axis_size("block")
+    to = {}
+    for g in range(groups):
+        for i in range(count):
+            to[g * count + i] = (g ^ 1) * count + i
+        for i in range(first, count - 1, 2):
+            to[g * count + i], to[g * count + i + 1] = g * count + i + 1, g * count + i
+    return lax.ppermute(x, ("partner", "block"), sorted(to.items()))
 
 
 def on_device(
@@ -300,6 +306,7 @@
     state = jax.ShapeDtypeStruct((leaves, vectors, LANES), jnp.float32)
     edge = jax.ShapeDtypeStruct((REACH, vectors, LANES), jnp.bfloat16)
     part = functools.partial
+    assert levels > 2
 
     sent = call(
         first_body,
@@ -317,7 +324,7 @@
     )(points, order, compress, block_map)
     received = from_partner(sent, levels - 1)
 
-    ordered, even, odd, table, mixers, dense = call(
+    ordered, even, odd, table, mixers, dense, expand = call(
         part(order_body, places),
         [
             jax.ShapeDtypeStruct((leaves, vectors, LANES), jnp.bfloat16),
@@ -326,17 +333,18 @@
             jax.ShapeDtypeStruct((places.rows, LANES), jnp.int32),
             jax.ShapeDtypeStruct(butterfly_mixers.shape, butterfly_mixers.dtype),
             jax.ShapeDtypeStruct(nearby_dense_blocks.shape, nearby_dense_blocks.dtype),
+            jax.ShapeDtypeStruct(expand.shape, expand.dtype),
         ],
-        [VMEM, VMEM, HBM, HBM, HBM, HBM],
+        [VMEM, VMEM, HBM, HBM, HBM, HBM, HBM],
         [
             pltpu.SMEM(block_map.shape, block_map.dtype),
             pltpu.SMEM((near_count, leaves), neighbours.dtype),
             ints,
             ints,
-            pltpu.SemaphoreType.DMA((4,)),
+            pltpu.SemaphoreType.DMA((5,)),
         ],
         flops=1 << 24,
-    )(points, order, block_map, neighbours.T, butterfly_mixers, nearby_dense_blocks)
+    )(points, order, block_map, neighbours.T, butterfly_mixers, nearby_dense_blocks, expand)
     even = with_neighbour(even, 0)
     odd = with_neighbour(odd, 1)
 
@@ -344,12 +352,14 @@
     own = call(part(top_own_body, places), state, [VMEM] * 4, flops=1 << 24)(
         table, received, top_factor, mixers
     )
-    field, place, joint = call(
+    wide = jax.ShapeDtypeStruct((leaves, LANES, 2 * LANES), jnp.bfloat16)
+    field, place, joint_own, joint = call(
         part(near_body, places),
         [
             state,
             jax.ShapeDtypeStruct((8, count), jnp.int32),
-            jax.ShapeDtypeStruct((leaves, LANES, 2 * LANES), jnp.bfloat16),
+            wide,
+            wide,
         ],
         [VMEM] * 8,
         [pltpu.VMEM((leaves + 2 * REACH, vectors, LANES), jnp.bfloat16)],
@@ -363,23 +373,19 @@
                 table, received, own, mixers
             )
             if level < levels - 2:
-                own = call(
-                    part(mix_own_body, places, level), state, [VMEM] * 4, flops=1 << 24
-                )(table, received, own, mixers)
-        if level == max(levels - 2, 1):
-            base = call(
-                part(base_body, places, level if levels > 2 else 0),
-                state,
-                [VMEM] * 6,
-                flops=1 << 24,
-            )(table, received, own, mixers, expand, field)
+                body, factors = mix_own_body, (mixers,)
+            else:
+                body, factors = base_body, (mixers, joint_own, field)
+            own = call(
+                part(body, places, level), state, [VMEM] * (3 + len(factors)), flops=1 << 24
+            )(table, received, own, *factors)
     return call(
         part(last_body, places, levels - 1),
         jax.ShapeDtypeStruct(points.shape, points.dtype),
         [VMEM] * 5,
         [pltpu.VMEM(points.shape, points.dtype), pltpu.SemaphoreType.DMA((4,))],
         place=HBM,
-    )(table, received, base, joint, place)
+    )(table, received, own, joint, place)
 
 
 def solution(mesh):

time: 21.5 us -> 18.7 us (0.87)
  starting transfers between devices: 6.76 us -> 4.86 us
  Pallas kernels: 7.3 us -> 6.44 us
    ppermute x2, starting transfers between devices: 3.55 us -> 1.64 us  [with_neighbour(): return lax.ppermute(x, ('partner', 'block'), sorted(to.items()))]
    pallas_call x8, Pallas kernels: 7.3 us -> 6.44 us  [bound(): run(*[pltpu.with_memory_space_constraint(a, pltpu.HBM) if s is HBM else a...]
  transfers between devices with their start and end apart: 5 -> 5, of which waited for: 4 -> 4; matrix products, arithmetic and copies ran while one was open for 0% -> 0% of each run, Pallas kernels for 21% -> 19%
where the time goes in v4:
time: 18.7 us; the launch traced here: 18.6 us
  waiting for transfers between devices  7.18 us (38%)
  Pallas kernels  6.44 us (34%)
  starting transfers between devices  4.86 us (26%)
    pallas_call x8, Pallas kernels, bound(): run(*[pltpu.with_memory_space_constraint(a, pltpu.HBM) if s is HBM else a...  6.44 us
    ppermute x2, waiting for transfers between devices, with_neighbour(): return lax.ppermute(x, ('partner', 'block'), sorted(to.items()))  3.74 us
    ppermute x3, waiting for transfers between devices, from_partner(): return lax.ppermute(x, 'partner', [(i, i ^ 1 << bit) for i in range(count)])  3.44 us
    ppermute x3, starting transfers between devices, from_partner(): return lax.ppermute(x, 'partner', [(i, i ^ 1 << bit) for i in range(count)])  3.21 us
    ppermute x2, starting transfers between devices, with_neighbour(): return lax.ppermute(x, ('partner', 'block'), sorted(to.items()))  1.64 us
  transfers between devices with their start and end apart: 5, of which 4 were waited for; matrix products, arithmetic and copies ran while one was open for 0% of the time, Pallas kernels for 19%

profile of v4, /device:TPU:16, one launch (start us, length us, event | category | flops | bytes accessed | tf_op | source)
XLA Modules:
  0.0 18.6 jit_solution(621063893905800700)
XLA Ops:
  0.0 0.0 copy-start.1
  0.0 0.0 copy-start.2
  0.0 1.3 %shard_map.92 = bf16[4,64,128]{2,1,0:T(8,128)(2,1)S(1)} custom-call(bf16[32,1024]{1,0:T(8,128)(2,1)} %points.3, s32[8,128]{1,0:T(8,128)} %bitcast.2, bf16[8,128,128]{2,1,0:T(8,128)(2,1)} %compress.1, s32[3,8]{1,0:T(4,128)} %block_map.3), custom_call_target="tpu_custom_call" | custom-call | flops 1048576 | bytes 262144 | tf_op jit(solution)/shard_map/pallas_call | solution.py:30
  1.3 1.6 %collective-permute-start = (bf16[4,64,128]{2,1,0:T(8,128)(2,1)S(1)}, bf16[4,64,128]{2,1,0:T(8,128)(2,1)S(1)}, u32[]{:S(2)}, u32[]{:S(2)}) collective-permute-start(bf16[4,64,128]{2,1,0:T(8,128)(2,1)S(1)} %shard_map.92), channel_id=1, source_target_pairs={{0,16},{4,20},{8,24},{12,28},{16,0},{20,4},{24,8},{28,12},{1,17},{... | collective-permute-start | bytes 196616 | tf_op jit(solution)/shard_map/ppermute | solution.py:273
  2.9 0.0 copy-done.1
  2.9 0.0 copy-done.2
  2.9 0.0 copy-start
  2.9 1.7 %shard_map.91 = (bf16[8,32,128]{2,1,0:T(8,128)(2,1)S(1)}, bf16[2,32,128]{2,1,0:T(8,128)(2,1)S(1)}, bf16[2,32,128]{2,1,0:T(8,128)(2,1)S(1)}, s32[72,128]{1,0:T(8,...) custom-call(bf16[32,1024]{1,0:T(8,128)(2,1)S(1)} %copy-done.1, ...), custom_call_target="tpu_custom_call" | custom-call | flops 16777216 | bytes 262144 | tf_op jit(solution)/shard_map/pallas_call | solution.py:30
  4.5 1.1 %collective-permute-done.received = bf16[4,64,128]{2,1,0:T(8,128)(2,1)S(1)} collective-permute-done((bf16[4,64,128]{2,1,0:T(8,128)(2,1)S(1)}, bf16[4,64,128]{2,1,0:T(8,128)(2,1)S(1)}, u32[]{:S(2)}, u32[]{:S(2)}) %collective-permute-start) | collective-permute-done | bytes 65568 | tf_op jit(solution)/shard_map/ppermute | solution.py:273
  5.6 0.0 copy-done
  5.6 0.2 %shard_map.93 = bf16[4,64,128]{2,1,0:T(8,128)(2,1)S(1)} custom-call(s32[72,128]{1,0:T(8,128)S(1)} %get-tuple-element.16.table, bf16[4,64,128]{2,1,0:T(8,128)(2,1)S(1)} %collective-permute-done.received, bf16[8,128,128]{2,1,0:T(8,128)(2,1)S(1)} %copy-done), custom_call_target="tpu_custom_call" | custom-call | flops 1048576 | bytes 262144 | tf_op jit(solution)/shard_map/pallas_call | solution.py:30
  5.8 1.6 %collective-permute-start.1 = (bf16[4,64,128]{2,1,0:T(8,128)(2,1)S(1)}, bf16[4,64,128]{2,1,0:T(8,128)(2,1)S(1)}, u32[]{:S(2)}, u32[]{:S(2)}) collective-permute-start(bf16[4,64,128]{2,1,0:T(8,128)(2,1)S(1)} %shard_map.93), channel_id=1, source_target_pairs={{0,8},{4,12},{8,0},{12,4},{16,24},{20,28},{24,16},{28,20},{1,9},{5... | collective-permute-start | bytes 196616 | tf_op jit(solution)/shard_map/ppermute | solution.py:273
  7.4 0.4 %shard_map.94.own = f32[8,32,128]{2,1,0:T(8,128)S(1)} custom-call(s32[72,128]{1,0:T(8,128)S(1)} %get-tuple-element.16.table, bf16[4,64,128]{2,1,0:T(8,128)(2,1)S(1)} %collective-permute-done.received, bf16[8,128,128]{2,1,0:T(8,128)(2,1)S(1)} %copy-done, bf16[2,8,2,128,128]{4,3,2,1,0:T(8,128)(2,1)S(1)} %get-tuple-element.17.mixers), custom_call_target="tpu_custom_call" | custom-call | flops 16777216 | bytes 262144 | tf_op jit(solution)/shard_map/pallas_call | solution.py:30
  7.8 2.4 %collective-permute-done.1.received = bf16[4,64,128]{2,1,0:T(8,128)(2,1)S(1)} collective-permute-done((bf16[4,64,128]{2,1,0:T(8,128)(2,1)S(1)}, bf16[4,64,128]{2,1,0:T(8,128)(2,1)S(1)}, u32[]{:S(2)}, u32[]{:S(2)}) %collective-permute-start.1) | collective-permute-done | bytes 65568 | tf_op jit(solution)/shard_map/ppermute | solution.py:273
  10.1 0.2 %shard_map.95 = bf16[4,64,128]{2,1,0:T(8,128)(2,1)S(1)} custom-call(s32[72,128]{1,0:T(8,128)S(1)} %get-tuple-element.16.table, bf16[4,64,128]{2,1,0:T(8,128)(2,1)S(1)} %collective-permute-done.1.received, f32[8,32,128]{2,1,0:T(8,128)S(1)} %shard_map.94.own, bf16[2,8,2,128,128]{4,3,2,1,0:T(8,128)(2,1)S(1)} %get-tuple-element.17.mixers), custom_call_target="tpu_custom_call" | custom-call | flops 1048576 | bytes 262144 | tf_op jit(solution)/shard_map/pallas_call | solution.py:30
  10.3 0.1 collective-permute-start.2
  10.4 1.6 %collective-permute-start.3 = (bf16[2,32,128]{2,1,0:T(8,128)(2,1)S(1)}, bf16[2,32,128]{2,1,0:T(8,128)(2,1)S(1)}, u32[]{:S(2)}, u32[]{:S(2)}) collective-permute-start(bf16[2,32,128]{2,1,0:T(8,128)(2,1)S(1)} %get-tuple-element.18), channel_id=1, source_target_pairs={{0,1},{1,0},{2,3},{3,2},{4,5},{5,4},{6,7},{7,6},{8,9},{9,8},{10,11... | collective-permute-start | bytes 49160 | tf_op jit(solution)/shard_map/ppermute | solution.py:284
  12.1 0.0 collective-permute-start.4
  12.1 2.2 %collective-permute-done.3.even = bf16[2,32,128]{2,1,0:T(8,128)(2,1)S(1)} collective-permute-done((bf16[2,32,128]{2,1,0:T(8,128)(2,1)S(1)}, bf16[2,32,128]{2,1,0:T(8,128)(2,1)S(1)}, u32[]{:S(2)}, u32[]{:S(2)}) %collective-permute-start.3) | collective-permute-done | bytes 16416 | tf_op jit(solution)/shard_map/ppermute | solution.py:284
  14.2 1.6 %collective-permute-done.4.odd = bf16[2,32,128]{2,1,0:T(8,128)(2,1)S(1)} collective-permute-done((bf16[2,32,128]{2,1,0:T(8,128)(2,1)S(1)}, bf16[2,32,128]{2,1,0:T(8,128)(2,1)S(1)}, u32[]{:S(2)}, u32[]{:S(2)}) %collective-permute-start.4) | collective-permute-done | bytes 16416 | tf_op jit(solution)/shard_map/ppermute | solution.py:284
  15.8 1.1 %shard_map.96 = (f32[8,32,128]{2,1,0:T(8,128)S(1)}, s32[8,1024]{1,0:T(8,128)S(1)}, bf16[8,128,256]{2,1,0:T(8,128)(2,1)S(1)}, bf16[8,128,256]{2,1,0:T(8,128)(2,1)S(1)}) custom-call(s32[72,128]{1,0:T(8,128)S(1)} %get-tuple-element.16.table, bf16[2,32,128]{2,1,0:T(8,128)(2,1)S(1)} %collective-permute-done.3.even, ...), custom_call_target="tpu_custom_call" | custom-call | flops 33554432 | bytes 262144 | tf_op jit(solution)/shard_map/pallas_call | solution.py:30
  16.9 0.4 %shard_map.97.base = f32[8,32,128]{2,1,0:T(8,128)S(1)} custom-call(s32[72,128]{1,0:T(8,128)S(1)} %get-tuple-element.16.table, bf16[4,64,128]{2,1,0:T(8,128)(2,1)S(1)} %collective-permute-done.1.received, f32[8,32,128]{2,1,0:T(8,128)S(1)} %shard_map.94.own, bf16[2,8,2,128,128]{4,3,2,1,0:T(8,128)(2,1)S(1)} %get-tuple-element.17.mixers, ...), custom_call_target="tpu_custom_call" | custom-call | flops 16777216 | bytes 262144 | tf_op jit(solution)/shard_map/pallas_call | solution.py:30
  17.3 0.0 collective-permute-done.2.received
  17.3 1.2 %shard_map.98 = bf16[32,1024]{1,0:T(8,128)(2,1)} custom-call(s32[72,128]{1,0:T(8,128)S(1)} %get-tuple-element.16.table, bf16[4,64,128]{2,1,0:T(8,128)(2,1)S(1)} %collective-permute-done.2.received, f32[8,32,128]{2,1,0:T(8,128)S(1)} %shard_map.97.base, bf16[8,128,256]{2,1,0:T(8,128)(2,1)S(1)} %get-tuple-element.25.joint, s32[8,1024]{1,0:T(8,128)S(1)} %get-tuple-element.26.place), custom_call_target="tpu_custom_call" | custom-call | flops 1048576 | bytes 262144 | tf_op jit(solution)/shard_map/pallas_call | solution.py:30
Async XLA Ops:
  0.0 2.9 %copy-start.1 = (bf16[32,1024]{1,0:T(8,128)(2,1)S(1)}, bf16[32,1024]{1,0:T(8,128)(2,1)}, u32[]{:S(2)}) copy-start(bf16[32,1024]{1,0:T(8,128)(2,1)} %points.3) | copy-start | bytes 196612
  0.0 2.9 %copy-start.2 = (s32[1024]{0:T(1024)S(1)}, s32[1024]{0:T(1024)}, u32[]{:S(2)}) copy-start(s32[1024]{0:T(1024)} %param.10) | copy-start | bytes 12292
  1.3 4.3 %collective-permute-start = (bf16[4,64,128]{2,1,0:T(8,128)(2,1)S(1)}, bf16[4,64,128]{2,1,0:T(8,128)(2,1)S(1)}, u32[]{:S(2)}, u32[]{:S(2)}) collective-permute-start(bf16[4,64,128]{2,1,0:T(8,128)(2,1)S(1)} %shard_map.92), channel_id=1, source_target_pairs={{0,16},{4,20},{8,24},{12,28},{16,0},{20,4},{24,8},{28,12},{1,17},{... | collective-permute-start | bytes 196616 | tf_op jit(solution)/shard_map/ppermute | solution.py:273
  2.9 2.7 %copy-start = (bf16[8,128,128]{2,1,0:T(8,128)(2,1)S(1)}, bf16[8,128,128]{2,1,0:T(8,128)(2,1)}, u32[]{:S(2)}) copy-start(bf16[8,128,128]{2,1,0:T(8,128)(2,1)} %factor.3) | copy-start | bytes 786436
  5.8 4.3 %collective-permute-start.1 = (bf16[4,64,128]{2,1,0:T(8,128)(2,1)S(1)}, bf16[4,64,128]{2,1,0:T(8,128)(2,1)S(1)}, u32[]{:S(2)}, u32[]{:S(2)}) collective-permute-start(bf16[4,64,128]{2,1,0:T(8,128)(2,1)S(1)} %shard_map.93), channel_id=1, source_target_pairs={{0,8},{4,12},{8,0},{12,4},{16,24},{20,28},{24,16},{28,20},{1,9},{5... | collective-permute-start | bytes 196616 | tf_op jit(solution)/shard_map/ppermute | solution.py:273
  10.3 7.0 %collective-permute-start.2 = (bf16[4,64,128]{2,1,0:T(8,128)(2,1)S(1)}, bf16[4,64,128]{2,1,0:T(8,128)(2,1)S(1)}, u32[]{:S(2)}, u32[]{:S(2)}) collective-permute-start(bf16[4,64,128]{2,1,0:T(8,128)(2,1)S(1)} %shard_map.95), channel_id=1, source_target_pairs={{0,4},{4,0},{8,12},{12,8},{16,20},{20,16},{24,28},{28,24},{1,5},{5... | collective-permute-start | bytes 196616 | tf_op jit(solution)/shard_map/ppermute | solution.py:273
  10.4 3.8 %collective-permute-start.3 = (bf16[2,32,128]{2,1,0:T(8,128)(2,1)S(1)}, bf16[2,32,128]{2,1,0:T(8,128)(2,1)S(1)}, u32[]{:S(2)}, u32[]{:S(2)}) collective-permute-start(bf16[2,32,128]{2,1,0:T(8,128)(2,1)S(1)} %get-tuple-element.18), channel_id=1, source_target_pairs={{0,1},{1,0},{2,3},{3,2},{4,5},{5,4},{6,7},{7,6},{8,9},{9,8},{10,11... | collective-permute-start | bytes 49160 | tf_op jit(solution)/shard_map/ppermute | solution.py:284
  12.1 3.7 %collective-permute-start.4 = (bf16[2,32,128]{2,1,0:T(8,128)(2,1)S(1)}, bf16[2,32,128]{2,1,0:T(8,128)(2,1)S(1)}, u32[]{:S(2)}, u32[]{:S(2)}) collective-permute-start(bf16[2,32,128]{2,1,0:T(8,128)(2,1)S(1)} %get-tuple-element.20), channel_id=1, source_target_pairs={{0,4},{1,2},{2,1},{3,7},{4,0},{5,6},{6,5},{7,3},{8,12},{9,10},{10,... | collective-permute-start | bytes 49160 | tf_op jit(solution)/shard_map/ppermute | solution.py:284
